TPU v7x, 32 devices: a whole 2x2x4 slice. The times are simulated.
32 devices in a mesh: grid: 2 (over core), px: 4 (over y, x), py: 4 (over z).
Axes of the slice: x: 2, y: 2, z: 4, core: 2. Of those that a mesh axis runs over, the one named last changes fastest.
Arguments:
- residual: float32 [2, 32, 32, 5, 1024], P('grid', 'px', 'py'), may hold values from -3 to 3
- inverses: float32 [2, 32, 32, 25, 1024], P('grid', 'px', 'py'), may hold values from 0 to 1, as said below
- couplings: float32 [2, 32, 32, 4, 1024], P('grid', 'px', 'py'), may hold values from 0.22 to 0.735, as said below
- receptors: int32 [2, 4, 4, 512], P('grid', 'px', 'py'), may hold values from 0 to 65535, as said below
- owners: int32 [2, 4, 4, 512, 1], P('grid', 'px', 'py'), may hold values from 0 to 15; in each aligned block of 512 rows (0 to 511, 512 to 1023, ..., all dimensions but the last counted through in order) at most 64 rows name the same one
- donors: int32 [2, 4, 4, 512, 8], P('grid', 'px', 'py'), may hold values from 0 to 65535
- weights: float32 [2, 4, 4, 512, 8], P('grid', 'px', 'py'), may hold values from 0 to 1, as said below
Outputs:
- update: float32 [2, 32, 32, 5, 1024], P('grid', 'px', 'py')
Inputs may be any that keep to these rules, and one draw needn't show every extreme that they name: `receptors`: receptor indices of one device are distinct. `owners`: among the receptors of one device no owner appears more than 64 times, and in every draw some device names one owner exactly 64 times. `weights`: nonnegative; the 8 weights of a receptor sum to 1. `inverses`: all entries nonnegative; off-diagonal entries 0.02 to 0.07; each row of a block sums to 0.94 to 1. `couplings`: a + b and e + f of each cell lie in 0.88 to 0.98, and each coupling is a quarter to three quarters of its pair's sum.
All inputs are finite; a program needn't handle non-finite values.
Results may differ from a plain program's by a relative error of at most 0.0001.
Values sent between devices are 32-bit elements; how exact they have to be, the bound alone decides.
A program may use at most 128 MiB of HBM per device.

v0:
```python
import functools

import jax
import jax.numpy as jnp
from jax import lax
from jax.experimental import pallas as pl
from jax.experimental.pallas import tpu as pltpu
from jax.sharding import PartitionSpec as P

MESH = pl.DeviceIdType.MESH
LANES = 128
INV_ROWS = 40
SMALL_ROWS = 8


def sweep_kernel(
    dims,
    res_hbm,
    inv_hbm,
    cpl_hbm,
    out_hbm,
    inv_v,
    res_v,
    cpl_v,
    skew_inv,
    skew_cpl,
    star_v,
    out_v,
    face_send,
    face_recv,
    in_sem,
    out_sem,
    send_sem,
    recv_sem,
):
    ci, cj, comps, blocks, count_rows, count_cols = dims
    steps = ci + cj - 1
    wide = cj + 2 * (ci - 1)
    px = lax.axis_index("px")
    py = lax.axis_index("py")

    def input_copies(kb):
        lanes = pl.ds(pl.multiple_of(kb * LANES, LANES), LANES)
        return (
            pltpu.make_async_copy(
                inv_hbm.at[:, :, lanes],
                inv_v.at[kb, :, pl.ds(0, comps * comps), :],
                in_sem.at[0, kb],
            ),
            pltpu.make_async_copy(
                res_hbm.at[:, :, lanes], res_v.at[kb, :, pl.ds(0, comps), :], in_sem.at[1, kb]
            ),
            pltpu.make_async_copy(
                cpl_hbm.at[:, :, lanes], cpl_v.at[kb, :, pl.ds(0, 4), :], in_sem.at[2, kb]
            ),
        )

    for kb in range(blocks):
        for copy in input_copies(kb):
            copy.start()

    has_prev_row = px > 0
    has_next_row = px < count_rows - 1
    has_prev_col = py > 0
    has_next_col = py < count_cols - 1
    prev_row = {"px": px - 1}
    next_row = {"px": px + 1}
    prev_col = {"py": py - 1}
    next_col = {"py": py + 1}
    sides = (
        (has_prev_row, prev_row),
        (has_next_row, next_row),
        (has_prev_col, prev_col),
        (has_next_col, next_col),
    )
    barrier = pltpu.get_barrier_semaphore()
    for there, device in sides:

        @pl.when(there)
        def _():
            pl.semaphore_signal(barrier, inc=1, device_id=device, device_id_type=MESH)

    pl.semaphore_wait(barrier, sum(there.astype(jnp.int32) for there, _ in sides))

    def send(kind, kb):
        device = (next_row, next_col, prev_row, prev_col)[kind]
        return pltpu.make_async_remote_copy(
            src_ref=face_send.at[kind, kb],
            dst_ref=face_recv.at[kind, kb],
            send_sem=send_sem.at[kind, kb],
            recv_sem=recv_sem.at[kind, kb],
            device_id=device,
            device_id_type=MESH,
        )

    gets = (has_prev_row, has_prev_col, has_next_row, has_next_col)
    puts = (has_next_row, has_next_col, has_prev_row, has_prev_col)

    for kind in range(4):

        @pl.when(jnp.logical_not(gets[kind]))
        def _():
            face_recv[kind] = jnp.zeros(face_recv.shape[1:], jnp.float32)

    sub = lax.broadcasted_iota(jnp.int32, (ci, LANES), 0)

    def product(mat, vec):
        out = []
        for r in range(comps):
            terms = [mat(r * comps + c) * vec[c] for c in range(comps)]
            while len(terms) > 1:
                terms = [
                    terms[t] + terms[t + 1] if t + 1 < len(terms) else terms[t]
                    for t in range(0, len(terms), 2)
                ]
            out.append(terms[0])
        return out

    def wait_recv(kind, kb):
        @pl.when(gets[kind])
        def _():
            send(kind, kb).wait_recv()

    def start_send(kind, kb):
        @pl.when(puts[kind])
        def _():
            send(kind, kb).start()

    inv_flat = inv_v.reshape(blocks, ci * cj * INV_ROWS, LANES)
    res_flat = res_v.reshape(blocks, ci * cj * SMALL_ROWS, LANES)
    cpl_flat = cpl_v.reshape(blocks, ci * cj * SMALL_ROWS, LANES)
    out_flat = out_v.reshape(blocks, ci * wide * SMALL_ROWS, LANES)

    def forward(kb):
        for copy in input_copies(kb):
            copy.wait()
        wait_recv(0, kb)
        wait_recv(1, kb)
        left_face = [face_recv[1, kb, pl.ds(c * ci, ci), :] for c in range(comps)]
        prev = [jnp.zeros((ci, LANES), jnp.float32)] * comps
        right = [jnp.zeros((ci, LANES), jnp.float32)] * comps
        for s in range(steps):

            def take(ref, rows, row):
                return ref[kb, pl.ds(s * rows + row, ci, stride=(cj - 1) * rows), :]

            coup = [take(cpl_flat, SMALL_ROWS, c) for c in range(4)]
            skew_cpl[kb, s, 0] = coup[2]
            skew_cpl[kb, s, 1] = coup[3]
            up = [pltpu.roll(p, 1, 0) for p in prev]
            if s < cj:
                up = [
                    jnp.where(
                        sub == 0,
                        jnp.broadcast_to(face_recv[0, kb, pl.ds(c * cj + s, 1), :], (ci, LANES)),
                        up[c],
                    )
                    for c in range(comps)
                ]
            left = prev
            if s < ci:
                left = [jnp.where(sub == s, left_face[c], prev[c]) for c in range(comps)]
            vec = [
                take(res_flat, SMALL_ROWS, c) + coup[0] * up[c] + coup[1] * left[c]
                for c in range(comps)
            ]

            def mat(e):
                value = take(inv_flat, INV_ROWS, e)
                skew_inv[kb, s, e] = value
                return value

            prev = product(mat, vec)
            for c in range(comps):
                star_v[kb, s, c] = prev[c]
                if s >= ci - 1:
                    face_send[0, kb, pl.ds(c * cj + s - ci + 1, 1), :] = prev[c][ci - 1 : ci, :]
                if s >= cj - 1:
                    right[c] = jnp.where(sub == s - cj + 1, prev[c], right[c])
        for c in range(comps):
            face_send[1, kb, pl.ds(c * ci, ci), :] = right[c]
        start_send(0, kb)
        start_send(1, kb)

    def out_copy(kb):
        return pltpu.make_async_copy(
            out_v.at[kb, :, pl.ds(ci - 1, cj), pl.ds(0, comps), :],
            out_hbm.at[:, :, kb, pl.ds(0, comps), :],
            out_sem.at[kb],
        )

    def backward(kb):
        wait_recv(2, kb)
        wait_recv(3, kb)
        right_face = [face_recv[3, kb, pl.ds(c * ci, ci), :] for c in range(comps)]
        prev = [jnp.zeros((ci, LANES), jnp.float32)] * comps
        left = [jnp.zeros((ci, LANES), jnp.float32)] * comps
        for s in reversed(range(steps)):
            down = [pltpu.roll(p, ci - 1, 0) for p in prev]
            if s >= ci - 1:
                down = [
                    jnp.where(
                        sub == ci - 1,
                        jnp.broadcast_to(
                            face_recv[2, kb, pl.ds(c * cj + s - ci + 1, 1), :], (ci, LANES)
                        ),
                        down[c],
                    )
                    for c in range(comps)
                ]
            right = prev
            if s >= cj - 1:
                right = [jnp.where(sub == s - cj + 1, right_face[c], prev[c]) for c in range(comps)]
            coup_e = skew_cpl[kb, s, 0]
            coup_f = skew_cpl[kb, s, 1]
            vec = [coup_e * down[c] + coup_f * right[c] for c in range(comps)]
            prev = product(lambda e: skew_inv[kb, s, e], vec)
            prev = [star_v[kb, s, c] + prev[c] for c in range(comps)]
            for c in range(comps):
                out_flat[
                    kb, pl.ds((s + ci - 1) * SMALL_ROWS + c, ci, stride=(wide - 1) * SMALL_ROWS), :
                ] = prev[c]
                if s < cj:
                    face_send[2, kb, pl.ds(c * cj + s, 1), :] = prev[c][0:1, :]
                if s < ci:
                    left[c] = jnp.where(sub == s, prev[c], left[c])
        for c in range(comps):
            face_send[3, kb, pl.ds(c * ci, ci), :] = left[c]
        start_send(2, kb)
        start_send(3, kb)
        out_copy(kb).start()

    reach = count_rows + count_cols - 2
    ahead = px + py
    behind = 2 * reach - ahead

    @pl.loop(0, 2 * reach + blocks)
    def _(n):
        @pl.when((n >= ahead) & (n < ahead + blocks))
        def _():
            forward(n - ahead)

        @pl.when((n >= behind) & (n < behind + blocks))
        def _():
            backward(n - behind)

    for kb in range(blocks):
        out_copy(kb).wait()
        for kind in range(4):

            @pl.when(puts[kind])
            def _():
                send(kind, kb).wait_send()


def run_sweeps(residual, inverses, couplings):
    ci, cj, comps, length = residual.shape
    blocks = length // LANES
    steps = ci + cj - 1
    wide = cj + 2 * (ci - 1)
    dims = (ci, cj, comps, blocks, lax.axis_size("px"), lax.axis_size("py"))
    face = comps * max(ci, cj)
    flat = lambda x: x.reshape((ci * cj,) + x.shape[2:])
    return pl.pallas_call(
        functools.partial(sweep_kernel, dims),
        out_shape=jax.ShapeDtypeStruct((ci, cj, blocks, SMALL_ROWS, LANES), jnp.float32),
        in_specs=[pl.BlockSpec(memory_space=pl.ANY)] * 3,
        out_specs=pl.BlockSpec(memory_space=pl.ANY),
        scratch_shapes=[
            pltpu.VMEM((blocks, ci * cj, INV_ROWS, LANES), jnp.float32),
            pltpu.VMEM((blocks, ci * cj, SMALL_ROWS, LANES), jnp.float32),
            pltpu.VMEM((blocks, ci * cj, SMALL_ROWS, LANES), jnp.float32),
            pltpu.VMEM((blocks, steps, comps * comps, ci, LANES), jnp.float32),
            pltpu.VMEM((blocks, steps, 2, ci, LANES), jnp.float32),
            pltpu.VMEM((blocks, steps, comps, ci, LANES), jnp.float32),
            pltpu.VMEM((blocks, ci, wide, SMALL_ROWS, LANES), jnp.float32),
            pltpu.VMEM((4, blocks, face, LANES), jnp.float32),
            pltpu.VMEM((4, blocks, face, LANES), jnp.float32),
            pltpu.SemaphoreType.DMA((3, blocks)),
            pltpu.SemaphoreType.DMA((blocks,)),
            pltpu.SemaphoreType.DMA((4, blocks)),
            pltpu.SemaphoreType.DMA((4, blocks)),
        ],
        compiler_params=pltpu.CompilerParams(
            collective_id=0, has_side_effects=True, vmem_limit_bytes=60 * 1024 * 1024
        ),
    )(flat(residual), flat(inverses), flat(couplings))


def swapped(array, axis, distance):
    return lax.ppermute(array, axis, [(i, i ^ 1 << distance) for i in range(lax.axis_size(axis))])


def split_dot(exact, value, dims):
    high = value.astype(jnp.bfloat16)
    low = (value - high.astype(jnp.float32)).astype(jnp.bfloat16)
    dot = lambda v: lax.dot_general(exact, v, dims, preferred_element_type=jnp.float32)
    return dot(high) + dot(low)


def plan_kernel(owner_count, slot_count, owners, donors, weights, place_out, packet_out):
    owner = owners[...]
    count = owner.shape[0]
    names = lax.broadcasted_iota(jnp.int32, (count, owner_count), 1)
    hit = owner == names
    ones = jnp.where(hit, 1.0, 0.0)
    row = lax.broadcasted_iota(jnp.int32, (count, count), 0)
    col = lax.broadcasted_iota(jnp.int32, (count, count), 1)
    before = jnp.where(col < row, 1.0, 0.0).astype(jnp.bfloat16)
    seen = jnp.dot(before, ones.astype(jnp.bfloat16), preferred_element_type=jnp.float32)
    rank = jnp.sum(seen * ones, axis=1, keepdims=True).astype(jnp.int32)
    place = owner * slot_count + rank
    place_out[...] = place
    slots = owner_count * slot_count
    slot = lax.broadcasted_iota(jnp.int32, (count, slots), 1)
    pick = jnp.where(slot == place, 1.0, 0.0).astype(jnp.bfloat16)
    over = (((0,), (0,)), ((), ()))
    cells = donors[...]
    both = jnp.concatenate(
        [(cells // LANES).astype(jnp.float32), (cells % LANES).astype(jnp.float32), weights[...]],
        axis=1,
    )
    high = both.astype(jnp.bfloat16)
    rest = both - high.astype(jnp.float32)
    mid = rest.astype(jnp.bfloat16)
    low = (rest - mid.astype(jnp.float32)).astype(jnp.bfloat16)
    dot = lambda v: lax.dot_general(pick, v, over, preferred_element_type=jnp.float32)
    packet_out[...] = (dot(high) + dot(mid)) + dot(low)


def run_plan(owner_count, slot_count, owners, donors, weights):
    count, many = donors.shape
    slots = owner_count * slot_count
    return pl.pallas_call(
        functools.partial(plan_kernel, owner_count, slot_count),
        out_shape=(
            jax.ShapeDtypeStruct((count, 1), jnp.int32),
            jax.ShapeDtypeStruct((slots, 3 * many), jnp.float32),
        ),
    )(owners, donors, weights)


def gather_kernel(many, rows, packet, field, out, spread):
    slots = packet.shape[0]
    lane = lax.broadcasted_iota(jnp.int32, (8, LANES), 1)

    tall = min(32, slots)

    @pl.loop(0, slots // tall)
    def _(t):
        at = pl.multiple_of(t * tall, 8)
        tile = packet[pl.ds(at, tall), :]
        line = lax.broadcasted_iota(jnp.int32, (tall, LANES), 1)
        for d in range(many):
            spot = tile[:, many + d : many + d + 1].astype(jnp.int32)
            spread[d, pl.ds(at, tall), :] = jnp.where(
                line == spot, tile[:, 2 * many + d : 2 * many + d + 1], 0.0
            )

    group = min(LANES, slots)
    turn = min(16, group)

    @pl.loop(0, slots // group)
    def _(g):
        def body(q, acc):
            first = g * group + q * turn
            for u in range(turn):
                parts = [
                    field[rows[(first + u) * many + d]] * spread[d, pl.ds(first + u, 1), :]
                    for d in range(many)
                ]
                while len(parts) > 1:
                    parts = [parts[i] + parts[i + 1] for i in range(0, len(parts), 2)]
                total = jnp.sum(parts[0], axis=1, keepdims=True)
                acc = jnp.where(lane == q * turn + u, total, acc)
            return acc

        acc = lax.fori_loop(0, group // turn, body, jnp.zeros((8, LANES), jnp.float32))
        out[:, pl.ds(pl.multiple_of(g * group, group), group)] = acc[:, :group]


def run_gather(packet, field):
    slots = packet.shape[0]
    many = packet.shape[1] // 3
    rows = packet[:, :many].astype(jnp.int32).reshape(-1)
    return pl.pallas_call(
        functools.partial(gather_kernel, many),
        out_shape=jax.ShapeDtypeStruct((8, slots), jnp.float32),
        in_specs=[
            pl.BlockSpec(memory_space=pltpu.SMEM),
            pl.BlockSpec(memory_space=pltpu.VMEM),
            pl.BlockSpec(memory_space=pltpu.VMEM),
        ],
        out_specs=pl.BlockSpec(memory_space=pltpu.VMEM),
        scratch_shapes=[pltpu.VMEM((many, slots, LANES), jnp.float32)],
        compiler_params=pltpu.CompilerParams(vmem_limit_bytes=40 * 1024 * 1024),
    )(rows, packet, field)


def place_kernel(place, returned, receptors, field, out):
    count, slots = place.shape[0], returned.shape[1]
    comps, blocks = out.shape[1], out.shape[2] // LANES
    slot = lax.broadcasted_iota(jnp.int32, (count, slots), 1)
    pick = jnp.where(slot == place[...], 1.0, 0.0).astype(jnp.bfloat16)
    value = returned[...]
    high = value.astype(jnp.bfloat16)
    low = (value - high.astype(jnp.float32)).astype(jnp.bfloat16)
    dims = (((1,), (1,)), ((), ()))
    row8 = lax.broadcasted_iota(jnp.int32, (8, count), 0)

    def chosen(piece, marker):
        got = lax.dot_general(piece, pick, dims, preferred_element_type=jnp.float32)
        return jnp.where(row8 == comps, marker, got)

    high_of = chosen(high, 1.0)
    low_of = chosen(low, 0.0)
    cell = receptors[...]
    tile = cell // LANES
    lane = lax.broadcasted_iota(jnp.int32, (LANES, count), 0)
    spots = jnp.where(lane == cell % LANES, 1.0, 0.0).astype(jnp.bfloat16)
    pencils = 8

    @pl.loop(0, out.shape[0] // pencils)
    def _(g):
        for kb in range(blocks):
            parts_high, parts_low = [], []
            for p in range(pencils):
                here = jnp.broadcast_to(tile == (g * pencils + p) * blocks + kb, (8, count))
                parts_high.append(jnp.where(here, high_of, 0.0))
                parts_low.append(jnp.where(here, low_of, 0.0))
            stack_high = jnp.concatenate(parts_high, axis=0).astype(jnp.bfloat16)
            stack_low = jnp.concatenate(parts_low, axis=0).astype(jnp.bfloat16)
            put = lax.dot_general(
                stack_high, spots, dims, preferred_element_type=jnp.float32
            ) + lax.dot_general(stack_low, spots, dims, preferred_element_type=jnp.float32)
            lanes = pl.ds(kb * LANES, LANES)
            for p in range(pencils):
                new = put[p * 8 : p * 8 + comps, :]
                mark = jnp.broadcast_to(put[p * 8 + comps : p * 8 + comps + 1, :], (comps, LANES))
                at = g * pencils + p
                out[at, :, lanes] = jnp.where(mark > 0.5, new, field[at * blocks + kb, pl.ds(0, comps), :])


def run_place(place, returned, receptors, field, shape):
    return pl.pallas_call(
        place_kernel,
        out_shape=jax.ShapeDtypeStruct(shape, jnp.float32),
        compiler_params=pltpu.CompilerParams(vmem_limit_bytes=40 * 1024 * 1024),
    )(place, returned, receptors, field)


def local(residual, inverses, couplings, receptors, owners, donors, weights):
    ci, cj, comps, length = residual.shape[1:]
    owner_count = lax.axis_size("px") * lax.axis_size("py")
    many = donors.shape[-1]
    count = donors.shape[-2]
    slot_count = max(2, 2 * count // owner_count)
    slots = owner_count * slot_count
    place, packet = run_plan(
        owner_count,
        slot_count,
        owners.reshape(count, 1),
        donors.reshape(count, many),
        weights.reshape(count, many),
    )
    packet = swapped(packet, "grid", 0).reshape(owner_count, slot_count, 3 * many)
    packet = lax.all_to_all(packet, ("px", "py"), split_axis=0, concat_axis=0, tiled=True)
    packet = packet.reshape(slots, 3 * many)
    swept = run_sweeps(residual[0], inverses[0], couplings[0])
    field = swept.reshape((-1,) + swept.shape[-2:])
    values = run_gather(packet, field)[:comps]
    values = values.reshape(comps, owner_count, slot_count).transpose(1, 0, 2)
    values = lax.all_to_all(values, ("px", "py"), split_axis=0, concat_axis=0, tiled=True)
    values = swapped(values, "grid", 0)
    values = jnp.pad(values.transpose(1, 0, 2).reshape(comps, slots), ((0, 8 - comps), (0, 0)))
    update = run_place(
        place, values, receptors.reshape(1, count), field, (ci * cj, comps, length)
    )
    return update.reshape(1, ci, cj, comps, length)


def solution(mesh):
    placed = (
        P("grid", "px", "py", None, None),
        P("grid", "px", "py", None, None),
        P("grid", "px", "py", None, None),
        P("grid", "px", "py", None),
        P("grid", "px", "py", None, None),
        P("grid", "px", "py", None, None),
        P("grid", "px", "py", None, None),
    )
    return jax.shard_map(
        local,
        mesh=mesh,
        in_specs=placed,
        out_specs=P("grid", "px", "py", None, None),
        check_vma=False,
    )
```

profile of v0, /device:TPU:0, one launch (start us, length us, event | category | flops | bytes accessed | tf_op | source)
XLA Modules:
  0.0 138.6 jit_solution(6301560474543699986)
XLA Ops:
  0.0 1.6 %copy.21.owners = s32[512,1]{1,0:T(8,128)} copy(s32[512,1]{0,1:T(1,128)} %bitcast.35) | data formatting | bytes 4096 | tf_op jit(solution)/shard_map/reshape | solution.py:462
  1.6 1.5 %copy.19 = s32[1,1,1,512,8]{4,3,2,1,0:T(8,128)} copy(s32[1,1,1,512,8]{3,4,2,1,0:T(8,128)} %param.12) | data formatting | bytes 32768 | tf_op args[5]
  3.2 1.5 %copy.20 = f32[1,1,1,512,8]{4,3,2,1,0:T(8,128)} copy(f32[1,1,1,512,8]{3,4,2,1,0:T(8,128)} %param.13) | data formatting | bytes 32768 | tf_op args[6]
  4.7 3.9 %shard_map.73 = (s32[512,1]{1,0:T(8,128)}, f32[1024,24]{1,0:T(8,128)}) custom-call(s32[512,1]{1,0:T(8,128)} %copy.21.owners, s32[512,8]{1,0:T(8,128)} %bitcast.27, f32[512,8]{1,0:T(8,128)} %bitcast.28), custom_call_target="tpu_custom_call" | custom-call | tf_op jit(solution)/shard_map/pallas_call | solution.py:334
  8.6 0.5 collective-permute-start
  9.1 1.7 %collective-permute-done = f32[1024,24]{1,0:T(8,128)S(1)} collective-permute-done((f32[1024,24]{1,0:T(8,128)}, f32[1024,24]{1,0:T(8,128)S(1)}, u32[]{:S(2)}, u32[]{:S(2)}) %collective-permute-start) | collective-permute-done | bytes 98336 | tf_op jit(solution)/shard_map/ppermute | solution.py:291
  10.9 0.2 copy.22
  11.1 0.8 reshape.44
  11.9 8.2 %all-to-all-start = ((f32[16,1,1536]{2,1,0:T(1,128)}), f32[16,1,1536]{2,1,0:T(1,128)S(1)}, u32[]{:S(2)}, u32[]{:S(2)}) async-start(f32[16,1,1536]{2,1,0:T(1,128)} %reshape.44), calls=%async_computation | async-start | bytes 196608 | tf_op jit(solution)/shard_map/all_to_all | solution.py:467
  20.1 2.1 %copy.24 = f32[1,8,8,5,1024]{4,3,2,1,0:T(8,128)} copy(f32[1,8,8,5,1024]{4,2,3,1,0:T(8,128)S(1)} %copy-done.3) | data formatting | bytes 2621440 | tf_op args[0]
  22.2 10.3 %copy.25 = f32[1,8,8,25,1024]{4,3,2,1,0:T(8,128)} copy(f32[1,8,8,25,1024]{4,2,3,1,0:T(8,128)} %param.8) | data formatting | bytes 13107200 | tf_op args[1]
  32.5 62.3 %shard_map.74 = f32[8,8,8,8,128]{4,3,2,1,0:T(8,128)} custom-call(f32[64,5,1024]{2,1,0:T(8,128)} %bitcast.26, f32[64,25,1024]{2,1,0:T(8,128)} %bitcast.25, f32[64,4,1024]{2,1,0:T(4,128)} %bitcast.29), custom_call_target="tpu_custom_call" | custom-call | tf_op jit(solution)/shard_map/pallas_call | solution.py:264
  94.9 0.5 broadcast.2
  95.4 1.0 reduce
  96.3 0.1 reshape.45
  96.4 0.2 copy.23
  96.7 0.3 reshape.38.rows
  97.0 19.9 %shard_map.75 = f32[8,1024]{1,0:T(8,128)S(1)} custom-call(s32[8192]{0:T(1024)S(1)} %reshape.38.rows, f32[1024,24]{1,0:T(8,128)S(1)} %bitcast.22, f32[512,8,128]{2,1,0:T(8,128)S(1)} %bitcast.18), custom_call_target="tpu_custom_call" | custom-call | tf_op jit(solution)/shard_map/pallas_call | solution.py:386
  117.0 0.1 reshape.46
  117.1 9.9 %all_to_all.10 = f32[16,1,320]{2,1,0:T(1,128)S(1)} all-to-all(f32[16,1,320]{2,1,0:T(1,128)S(1)} %reshape.46), channel_id=1, replica_groups=mesh['grid'=2,'px'=4,'py'=4] {'px','py'}, dimensions={0} | all-to-all | bytes 40960 | tf_op jit(solution)/shard_map/all_to_all | solution.py:473
  127.0 0.7 reduce.1
  127.8 1.2 collective-permute-done.1
  129.2 7.5 %shard_map.76 = f32[64,5,1024]{2,1,0:T(8,128)S(1)} custom-call(s32[512,1]{1,0:T(8,128)S(1)} %copy-done.1, f32[8,1024]{1,0:T(8,128)S(1)} %pad.4.returned, s32[1,512]{1,0:T(1,128)S(1)} %bitcast.24, f32[512,8,128]{2,1,0:T(8,128)S(1)} %bitcast.19), custom_call_target="tpu_custom_call" | custom-call | tf_op jit(solution)/shard_map/pallas_call | solution.py:445
  136.7 1.8 %copy.28 = f32[1,8,8,5,1024]{4,2,3,1,0:T(8,128)} copy(f32[1,8,8,5,1024]{4,3,2,1,0:T(8,128)S(1)} %bitcast.20) | data formatting | bytes 2621440 | tf_op jit(solution)/shard_map/reshape | solution.py:479
  (17 shorter events, 0.3 us)
Async XLA Ops:
  0.0 20.1 %copy-start.3 = (f32[1,8,8,5,1024]{4,2,3,1,0:T(8,128)S(1)}, f32[1,8,8,5,1024]{4,2,3,1,0:T(8,128)}, u32[]{:S(2)}) copy-start(f32[1,8,8,5,1024]{4,2,3,1,0:T(8,128)} %param.7) | copy-start | bytes 3932164
  8.6 2.2 %collective-permute-start = (f32[1024,24]{1,0:T(8,128)}, f32[1024,24]{1,0:T(8,128)S(1)}, u32[]{:S(2)}, u32[]{:S(2)}) collective-permute-start(f32[1024,24]{1,0:T(8,128)} %get-tuple-element.8), channel_id=1, source_target_pairs={{0,16},{16,0},{1,17},{17,1},{2,18},{18,2},{3,19},{19,3},{4,20},{20... | collective-permute-start | bytes 294920 | tf_op jit(solution)/shard_map/ppermute | solution.py:291
  11.9 83.0 %all-to-all-start = ((f32[16,1,1536]{2,1,0:T(1,128)}), f32[16,1,1536]{2,1,0:T(1,128)S(1)}, u32[]{:S(2)}, u32[]{:S(2)}) async-start(f32[16,1,1536]{2,1,0:T(1,128)} %reshape.44), calls=%async_computation | async-start | bytes 196608 | tf_op jit(solution)/shard_map/all_to_all | solution.py:467
  94.8 2.1 %copy-start = (f32[8,8,8,8,128]{4,3,2,1,0:T(8,128)S(1)}, f32[8,8,8,8,128]{4,3,2,1,0:T(8,128)}, u32[]{:S(2)}) copy-start(f32[8,8,8,8,128]{4,3,2,1,0:T(8,128)} %shard_map.74) | copy-start | bytes 6291460
  96.7 32.5 %copy-start.1 = (s32[512,1]{1,0:T(8,128)S(1)}, s32[512,1]{1,0:T(8,128)}, u32[]{:S(2)}) copy-start(s32[512,1]{1,0:T(8,128)} %get-tuple-element.7.place) | copy-start | bytes 6148
  96.7 32.5 %copy-start.2 = (s32[1,1,1,512]{3,2,1,0:T(1,128)S(1)}, s32[1,1,1,512]{3,2,1,0:T(1,128)}, u32[]{:S(2)}) copy-start(s32[1,1,1,512]{3,2,1,0:T(1,128)} %param.10) | copy-start | bytes 6148
  127.8 1.3 collective-permute-start.1
where the time goes:
time: 139 us
  Pallas kernels  93.7 us (67%)
  local copies, waits for them, and re-layouts  21.4 us (15%)
  blocking collectives  9.91 us (7%)
  starting transfers between devices  8.73 us (6%)
  waiting for transfers between devices  2.99 us (2%)
  other arithmetic  1.71 us (1%)
    pallas_call x1, Pallas kernels, run_sweeps(): pl.pallas_call(functools.partial(sweep_kernel, dims), out_shape=jax.Shape...  62.3 us
    pallas_call x1, Pallas kernels, run_gather(): pl.pallas_call(functools.partial(gather_kernel, many), out_shape=jax.Shap...  19.9 us
    unnamed x16, local copies, waits for them, and re-layouts  16.6 us
    all_to_all x1, blocking collectives, local(): lax.all_to_all(values, ('px', 'py'), split_axis=0, concat_axis=0, tiled=T...  9.91 us
    all_to_all x1, starting transfers between devices, local(): lax.all_to_all(packet, ('px', 'py'), split_axis=0, concat_axis=0, tiled=T...  8.22 us
    pallas_call x1, Pallas kernels, run_place(): pl.pallas_call(place_kernel, out_shape=jax.ShapeDtypeStruct(shape, jnp.fl...  7.51 us
    pallas_call x1, Pallas kernels, run_plan(): pl.pallas_call(functools.partial(plan_kernel, owner_count, slot_count), o...  3.92 us
    ppermute x2, waiting for transfers between devices, swapped(): lax.ppermute(array, axis, [(i, i ^ 1 << distance) for i in range(lax.axis...  2.99 us
  transfers between devices with their start and end apart: 3, of which 2 were waited for; matrix products, arithmetic and copies ran while one was open for 9% of the time, Pallas kernels for 45%

commit v1 on v0

v1 whole, which is shorter than its diff:
```python
import functools

import jax
import jax.numpy as jnp
from jax import lax
from jax.experimental import pallas as pl
from jax.experimental.pallas import tpu as pltpu
from jax.sharding import PartitionSpec as P

MESH = pl.DeviceIdType.MESH
LANES = 128
ROWS = 8
LOW = 8
EMPTY = LANES


def divmod_const(value, by):
    if by & (by - 1) == 0:
        return value >> (by.bit_length() - 1), value & (by - 1)
    return value // by, value % by


def sweep_kernel(
    dims,
    res_hbm,
    inv_hbm,
    cpl_hbm,
    owners,
    donors,
    weights,
    receptors,
    out_hbm,
    code_out,
    reply_out,
    inv_v,
    res_v,
    cpl_v,
    star_v,
    field_v,
    face_send,
    face_recv,
    ask_send,
    ask_recv,
    rows_v,
    rows_s,
    spread,
    reply_send,
    reply_recv,
    in_sem,
    out_sem,
    send_sem,
    recv_sem,
    ask_send_sem,
    ask_recv_sem,
    reply_send_sem,
    reply_recv_sem,
    rows_sem,
):
    ci, cj, comps, blocks, count_rows, count_cols, slot_count = dims
    length = blocks * LANES
    entries = comps * comps
    steps = ci + cj - 1
    tall = ci + 2 * (cj - 1)
    many, count = donors.shape
    owner_count = count_rows * count_cols
    slots = owner_count * slot_count
    grid = lax.axis_index("grid")
    px = lax.axis_index("px")
    py = lax.axis_index("py")
    me = px * count_cols + py
    ahead = px + py
    reach = count_rows + count_cols - 2

    def input_copies(kb):
        lanes = pl.ds(pl.multiple_of(kb * LANES, LANES), LANES)
        mine = pl.ds(cj - 1, ci)
        return (
            pltpu.make_async_copy(
                inv_hbm.at[:, :, :, lanes], inv_v.at[kb, mine], in_sem.at[0, kb]
            ),
            pltpu.make_async_copy(
                res_hbm.at[:, :, :, lanes], res_v.at[kb, mine], in_sem.at[1, kb]
            ),
            pltpu.make_async_copy(
                cpl_hbm.at[:, :, :, lanes],
                cpl_v.at[kb, mine, :, pl.ds(0, 4), :],
                in_sem.at[2, kb],
            ),
        )

    for kb in range(blocks):
        for copy in input_copies(kb):
            copy.start()

    has_prev_row = px > 0
    has_next_row = px < count_rows - 1
    has_prev_col = py > 0
    has_next_col = py < count_cols - 1
    prev_row = {"px": px - 1}
    next_row = {"px": px + 1}
    prev_col = {"py": py - 1}
    next_col = {"py": py + 1}
    sides = (
        (has_prev_row, prev_row),
        (has_next_row, next_row),
        (has_prev_col, prev_col),
        (has_next_col, next_col),
    )

    def other(q):
        return {"grid": 1 - grid, "px": q // count_cols, "py": q % count_cols}

    barrier = pltpu.get_barrier_semaphore()
    for there, device in sides:

        @pl.when(there)
        def _():
            pl.semaphore_signal(barrier, inc=1, device_id=device, device_id_type=MESH)

    @pl.loop(0, owner_count)
    def _(q):
        pl.semaphore_signal(barrier, inc=1, device_id=other(q), device_id_type=MESH)

    def enter():
        near = sum(there.astype(jnp.int32) for there, _ in sides)
        pl.semaphore_wait(barrier, near + owner_count)

    def ask(q):
        return pltpu.make_async_remote_copy(
            src_ref=ask_send.at[q],
            dst_ref=ask_recv.at[me],
            send_sem=ask_send_sem.at[q],
            recv_sem=ask_recv_sem.at[me],
            device_id=other(q),
            device_id_type=MESH,
        )

    def asked(q):
        return pltpu.make_async_remote_copy(
            src_ref=ask_send.at[q],
            dst_ref=ask_recv.at[q],
            send_sem=ask_send_sem.at[q],
            recv_sem=ask_recv_sem.at[q],
            device_id=other(q),
            device_id_type=MESH,
        )

    def reply(q):
        return pltpu.make_async_remote_copy(
            src_ref=reply_send.at[q],
            dst_ref=reply_recv.at[me],
            send_sem=reply_send_sem.at[q],
            recv_sem=reply_recv_sem.at[me],
            device_id=other(q),
            device_id_type=MESH,
        )

    def replied(q):
        return pltpu.make_async_remote_copy(
            src_ref=reply_send.at[q],
            dst_ref=reply_recv.at[q],
            send_sem=reply_send_sem.at[q],
            recv_sem=reply_recv_sem.at[q],
            device_id=other(q),
            device_id_type=MESH,
        )

    def digits(value):
        return [(value >> LOW).astype(jnp.float32), (value & (2**LOW - 1)).astype(jnp.float32)]

    def plan():
        owner = owners[...]
        ones = jnp.where(
            owner == lax.broadcasted_iota(jnp.int32, (owner_count, count), 0), 1.0, 0.0
        )
        before = jnp.where(
            lax.broadcasted_iota(jnp.int32, (count, count), 0)
            < lax.broadcasted_iota(jnp.int32, (count, count), 1),
            1.0,
            0.0,
        ).astype(jnp.bfloat16)
        seen = jnp.dot(ones.astype(jnp.bfloat16), before, preferred_element_type=jnp.float32)
        rank = jnp.sum(seen * ones, axis=0, keepdims=True).astype(jnp.int32)
        place = owner * slot_count + rank
        weight = weights[...]
        high = weight.astype(jnp.bfloat16).astype(jnp.float32)
        mid = (weight - high).astype(jnp.bfloat16).astype(jnp.float32)
        low = weight - high - mid
        cell = receptors[...]
        marks = jnp.concatenate(
            digits(cell) + [jnp.ones((1, count), jnp.float32), jnp.zeros((ROWS - 3, count), jnp.float32)],
            axis=0,
        )
        table = jnp.concatenate(digits(donors[...]) + [high, mid, low, marks], axis=0).astype(
            jnp.bfloat16
        )
        wide = min(2 * LANES, slots)
        lane = lax.broadcasted_iota(jnp.int32, (many, LANES), 1)
        for base in range(0, slots, wide):
            slot = lax.broadcasted_iota(jnp.int32, (wide, count), 0) + base
            pick = jnp.where(slot == place, 1.0, 0.0).astype(jnp.bfloat16)
            got = lax.dot_general(
                table, pick, (((1,), (1,)), ((), ())), preferred_element_type=jnp.float32
            )
            cells = got[:many] * float(2**LOW) + got[many : 2 * many]
            share = got[2 * many : 3 * many] + got[3 * many : 4 * many] + got[4 * many : 5 * many]
            mark = got[5 * many : 5 * many + 3]
            target = (mark[0:1] * float(2**LOW) + mark[1:2]).astype(jnp.int32)
            pencil, k = divmod_const(target, length)
            kb, spot = divmod_const(k, LANES)
            line = kb * (ci * cj) + pencil
            code_out[:, base : base + wide] = jnp.where(
                mark[2:3] > 0.5, line * (2 * LANES) + spot, EMPTY
            )
            for q in range(base // slot_count, (base + wide) // slot_count):
                at = q * slot_count - base
                tile = at // LANES * LANES
                shift = at - tile
                left = cells[:, tile : tile + LANES]
                right = share[:, tile : tile + LANES]
                if shift:
                    left = pltpu.roll(left, LANES - shift, 1)
                if (slot_count - shift) % LANES:
                    right = pltpu.roll(right, (slot_count - shift) % LANES, 1)
                ask_send[q] = jnp.where(lane < slot_count, left, right)

        @pl.when(ahead >= 2)
        def _():
            enter()

        @pl.loop(0, owner_count)
        def _(q):
            ask(q).start()

    def prepare():
        line = lax.broadcasted_iota(jnp.int32, (slot_count, LANES), 1)

        @pl.loop(0, owner_count)
        def _(q):
            asked(q).wait_recv()
            tile = ask_recv[q]
            cell = tile.astype(jnp.int32)
            pencil, k = divmod_const(cell, length)
            kb, _ = divmod_const(k, LANES)
            i, j = divmod_const(pencil, cj)
            row = kb * (tall * cj) + (i + (cj - 1)) * cj + j
            rows_v[pl.ds(pl.multiple_of(q * ROWS, ROWS), ROWS), :] = jnp.clip(
                row, 0, blocks * tall * cj - 1
            )
            turned = tile.T
            first = pl.multiple_of(q * slot_count, slot_count)
            for d in range(many):
                spot = turned[:slot_count, d : d + 1].astype(jnp.int32) & (LANES - 1)
                share = turned[slot_count : 2 * slot_count, d : d + 1]
                spread[d, pl.ds(first, slot_count), :] = jnp.where(line == spot, share, 0.0)

        copy = pltpu.make_async_copy(rows_v, rows_s, rows_sem)
        copy.start()
        copy.wait()

    def send(kind, kb):
        device = (next_row, next_col, prev_row, prev_col)[kind]
        return pltpu.make_async_remote_copy(
            src_ref=face_send.at[kind, kb],
            dst_ref=face_recv.at[kind, kb],
            send_sem=send_sem.at[kind, kb],
            recv_sem=recv_sem.at[kind, kb],
            device_id=device,
            device_id_type=MESH,
        )

    gets = (has_prev_row, has_prev_col, has_next_row, has_next_col)
    puts = (has_next_row, has_next_col, has_prev_row, has_prev_col)

    for kind in range(4):

        @pl.when(jnp.logical_not(gets[kind]))
        def _():
            face_recv[kind] = jnp.zeros(face_recv.shape[1:], jnp.float32)

    sub = lax.broadcasted_iota(jnp.int32, (cj, LANES), 0)

    def product(mat, vec):
        out = []
        for r in range(comps):
            terms = [mat(r * comps + c) * vec[c] for c in range(comps)]
            while len(terms) > 1:
                terms = [
                    terms[t] + terms[t + 1] if t + 1 < len(terms) else terms[t]
                    for t in range(0, len(terms), 2)
                ]
            out.append(terms[0])
        return out

    def wait_recv(kind, kb):
        @pl.when(gets[kind])
        def _():
            send(kind, kb).wait_recv()

    def start_send(kind, kb):
        @pl.when(puts[kind])
        def _():
            send(kind, kb).start()

    inv_flat = inv_v.reshape(blocks, tall * entries * cj, LANES)
    res_flat = res_v.reshape(blocks, tall * comps * cj, LANES)
    cpl_flat = cpl_v.reshape(blocks, tall * cj * ROWS, LANES)
    field_flat = field_v.reshape(blocks, tall * cj * ROWS, LANES)
    field_rows = field_v.reshape(blocks * tall * cj, ROWS, LANES)

    def entry(ref, kb, s, height, e):
        start = s * height * cj + e * cj + cj - 1
        return ref[kb, pl.ds(start, cj, stride=height * cj - 1), :]

    def cell_rows(s, c):
        return pl.ds((s * cj + cj - 1) * ROWS + c, cj, stride=(cj - 1) * ROWS)

    def forward(kb):
        for copy in input_copies(kb):
            copy.wait()
        wait_recv(0, kb)
        wait_recv(1, kb)
        upper = [face_recv[0, kb, pl.ds(c * ROWS, cj), :] for c in range(comps)]
        prev = [jnp.zeros((cj, LANES), jnp.float32)] * comps
        lower = [jnp.zeros((cj, LANES), jnp.float32)] * comps
        for s in range(steps):
            coef_a = cpl_flat[kb, cell_rows(s, 0), :]
            coef_b = cpl_flat[kb, cell_rows(s, 1), :]
            up = prev
            if s < cj:
                up = [jnp.where(sub == cj - 1 - s, upper[c], prev[c]) for c in range(comps)]
            left = [pltpu.roll(p, cj - 1, 0) for p in prev]
            if s < ci:
                left = [
                    jnp.where(
                        sub == cj - 1,
                        jnp.broadcast_to(
                            face_recv[1, kb, pl.ds(c * ROWS + s, 1), :], (cj, LANES)
                        ),
                        left[c],
                    )
                    for c in range(comps)
                ]
            vec = [
                entry(res_flat, kb, s, comps, c) + coef_a * up[c] + coef_b * left[c]
                for c in range(comps)
            ]
            prev = product(lambda e: entry(inv_flat, kb, s, entries, e), vec)
            for c in range(comps):
                star_v[kb, s, c] = prev[c]
                if s >= cj - 1:
                    face_send[1, kb, pl.ds(c * ROWS + s - cj + 1, 1), :] = prev[c][0:1, :]
                if s >= ci - 1:
                    lower[c] = jnp.where(sub == cj + ci - 2 - s, prev[c], lower[c])
        for c in range(comps):
            face_send[0, kb, pl.ds(c * ROWS, cj), :] = lower[c]

        @pl.when((kb == 0) & (ahead < 2))
        def _():
            enter()

        start_send(0, kb)
        start_send(1, kb)

    def out_copy(kb):
        return pltpu.make_async_copy(
            field_v.at[kb, pl.ds(cj - 1, ci)], out_hbm.at[kb], out_sem.at[kb]
        )

    def backward(kb):
        wait_recv(2, kb)
        wait_recv(3, kb)
        under = [face_recv[2, kb, pl.ds(c * ROWS, cj), :] for c in range(comps)]
        prev = [jnp.zeros((cj, LANES), jnp.float32)] * comps
        upper = [jnp.zeros((cj, LANES), jnp.float32)] * comps
        for s in reversed(range(steps)):
            coef_e = cpl_flat[kb, cell_rows(s, 2), :]
            coef_f = cpl_flat[kb, cell_rows(s, 3), :]
            down = prev
            if s >= ci - 1:
                down = [
                    jnp.where(sub == cj + ci - 2 - s, under[c], prev[c]) for c in range(comps)
                ]
            right = [pltpu.roll(p, 1, 0) for p in prev]
            if s >= cj - 1:
                right = [
                    jnp.where(
                        sub == 0,
                        jnp.broadcast_to(
                            face_recv[3, kb, pl.ds(c * ROWS + s - cj + 1, 1), :], (cj, LANES)
                        ),
                        right[c],
                    )
                    for c in range(comps)
                ]
            vec = [coef_e * down[c] + coef_f * right[c] for c in range(comps)]
            prev = product(lambda e: entry(inv_flat, kb, s, entries, e), vec)
            prev = [star_v[kb, s, c] + prev[c] for c in range(comps)]
            for c in range(comps):
                field_flat[kb, cell_rows(s, c), :] = prev[c]
                if s < cj:
                    upper[c] = jnp.where(sub == cj - 1 - s, prev[c], upper[c])
                if s < ci:
                    face_send[3, kb, pl.ds(c * ROWS + s, 1), :] = prev[c][cj - 1 : cj, :]
        for c in range(comps):
            face_send[2, kb, pl.ds(c * ROWS, cj), :] = upper[c]
        start_send(2, kb)
        start_send(3, kb)
        out_copy(kb).start()

    middle = blocks + 1
    last = 2 * blocks + 2
    begin = jnp.where(ahead == reach, 1, blocks + 2)
    early = ahead + 2 <= reach

    @pl.loop(0, last + 1)
    def _(n):
        @pl.when(((n == 0) & (ahead >= 2)) | ((n == middle) & (ahead < 2)))
        def _():
            plan()

        @pl.when((n >= 1) & (n <= blocks))
        def _():
            forward(n - 1)

        @pl.when((n >= begin) & (n < begin + blocks))
        def _():
            backward(n - begin)

        @pl.when(((n == middle) & early) | ((n == last) & jnp.logical_not(early)))
        def _():
            prepare()

    lane8 = lax.broadcasted_iota(jnp.int32, (ROWS, LANES), 1)
    turn = min(16, slot_count)

    @pl.loop(0, owner_count)
    def _(q):
        def body(t, acc):
            for u in range(turn):
                s = t * turn + u
                parts = [
                    field_rows[rows_s[q * ROWS + d, s]]
                    * spread[d, pl.ds(q * slot_count + s, 1), :]
                    for d in range(many)
                ]
                while len(parts) > 1:
                    parts = [parts[i] + parts[i + 1] for i in range(0, len(parts), 2)]
                total = jnp.sum(parts[0], axis=1, keepdims=True)
                acc = jnp.where(lane8 == s, total, acc)
            return acc

        reply_send[q] = lax.fori_loop(
            0, slot_count // turn, body, jnp.zeros((ROWS, LANES), jnp.float32)
        )
        reply(q).start()

    @pl.loop(0, owner_count)
    def _(q):
        replied(q).wait_recv()
        reply_out[q] = reply_recv[q]

    @pl.loop(0, owner_count)
    def _(q):
        ask(q).wait_send()
        reply(q).wait_send()

    for kb in range(blocks):
        out_copy(kb).wait()
        for kind in range(4):

            @pl.when(puts[kind])
            def _():
                send(kind, kb).wait_send()


def run_sweeps(residual, inverses, couplings, owners, donors, weights, receptors):
    ci, comps, cj, length = residual.shape
    many, count = donors.shape
    blocks = length // LANES
    steps = ci + cj - 1
    tall = ci + 2 * (cj - 1)
    rows, cols = lax.axis_size("px"), lax.axis_size("py")
    owner_count = rows * cols
    slot_count = max(2, 2 * count // owner_count)
    slots = owner_count * slot_count
    assert cj == ROWS and ci <= ROWS and many == ROWS and 2 * slot_count <= LANES
    assert ci * cj * length <= 2 ** (2 * LOW)
    dims = (ci, cj, comps, blocks, rows, cols, slot_count)
    face = comps * ROWS
    dma = pltpu.SemaphoreType.DMA
    hbm = pl.BlockSpec(memory_space=pl.ANY)
    vmem = pl.BlockSpec(memory_space=pltpu.VMEM)
    return pl.pallas_call(
        functools.partial(sweep_kernel, dims),
        out_shape=(
            jax.ShapeDtypeStruct((blocks, ci, cj, ROWS, LANES), jnp.float32),
            jax.ShapeDtypeStruct((1, slots), jnp.int32),
            jax.ShapeDtypeStruct((owner_count, ROWS, LANES), jnp.float32),
        ),
        in_specs=[hbm] * 3 + [vmem] * 4,
        out_specs=(hbm, vmem, vmem),
        scratch_shapes=[
            pltpu.VMEM((blocks, tall, comps * comps, cj, LANES), jnp.float32),
            pltpu.VMEM((blocks, tall, comps, cj, LANES), jnp.float32),
            pltpu.VMEM((blocks, tall, cj, ROWS, LANES), jnp.float32),
            pltpu.VMEM((blocks, steps, comps, cj, LANES), jnp.float32),
            pltpu.VMEM((blocks, tall, cj, ROWS, LANES), jnp.float32),
            pltpu.VMEM((4, blocks, face, LANES), jnp.float32),
            pltpu.VMEM((4, blocks, face, LANES), jnp.float32),
            pltpu.VMEM((owner_count, ROWS, LANES), jnp.float32),
            pltpu.VMEM((owner_count, ROWS, LANES), jnp.float32),
            pltpu.VMEM((owner_count * ROWS, LANES), jnp.int32),
            pltpu.SMEM((owner_count * ROWS, LANES), jnp.int32),
            pltpu.VMEM((many, slots, LANES), jnp.float32),
            pltpu.VMEM((owner_count, ROWS, LANES), jnp.float32),
            pltpu.VMEM((owner_count, ROWS, LANES), jnp.float32),
            dma((3, blocks)),
            dma((blocks,)),
            dma((4, blocks)),
            dma((4, blocks)),
            dma((owner_count,)),
            dma((owner_count,)),
            dma((owner_count,)),
            dma((owner_count,)),
            dma,
        ],
        compiler_params=pltpu.CompilerParams(
            collective_id=0, has_side_effects=True, vmem_limit_bytes=52 * 1024 * 1024
        ),
    )(residual, inverses, couplings, owners, donors, weights, receptors)


def place_kernel(dims, code, reply, field, out, work, sem):
    ci, cj, comps, blocks, slot_count = dims
    owner_count = reply.shape[0]
    copy = pltpu.make_async_copy(field, work, sem)
    copy.start()
    copy.wait()
    lane = lax.broadcasted_iota(jnp.int32, (ROWS, LANES), 1)
    lines = work.reshape(blocks * ci * cj, ROWS, LANES)

    @pl.loop(0, owner_count)
    def _(q):
        tile = reply[q]
        for s in range(slot_count):
            line, spot = divmod_const(code[0, q * slot_count + s], 2 * LANES)
            value = jnp.broadcast_to(tile[:, s : s + 1], (ROWS, LANES))
            pltpu.store(lines.at[line], value, mask=lane == spot)

    stack = work.reshape(blocks, ci, cj * ROWS, LANES)

    @pl.loop(0, ci)
    def _(i):
        for kb in range(blocks):
            for c in range(comps):
                out[i, c, :, kb * LANES : (kb + 1) * LANES] = stack[
                    kb, i, pl.ds(c, cj, stride=ROWS), :
                ]


def run_place(code, reply, field, slot_count, comps):
    blocks, ci, cj = field.shape[:3]
    return pl.pallas_call(
        functools.partial(place_kernel, (ci, cj, comps, blocks, slot_count)),
        out_shape=jax.ShapeDtypeStruct((ci, comps, cj, blocks * LANES), jnp.float32),
        in_specs=[
            pl.BlockSpec(memory_space=pltpu.SMEM),
            pl.BlockSpec(memory_space=pltpu.VMEM),
            pl.BlockSpec(memory_space=pl.ANY),
        ],
        out_specs=pl.BlockSpec(memory_space=pltpu.VMEM),
        scratch_shapes=[
            pltpu.VMEM(field.shape, jnp.float32),
            pltpu.SemaphoreType.DMA,
        ],
        compiler_params=pltpu.CompilerParams(vmem_limit_bytes=16 * 1024 * 1024),
    )(code, reply, field)


def local(residual, inverses, couplings, receptors, owners, donors, weights):
    comps = residual.shape[3]
    many = donors.shape[-1]
    count = donors.shape[-2]
    field, code, reply = run_sweeps(
        residual[0].transpose(0, 2, 1, 3),
        inverses[0].transpose(0, 2, 1, 3),
        couplings[0],
        owners.reshape(1, count),
        donors.reshape(count, many).T,
        weights.reshape(count, many).T,
        receptors.reshape(1, count),
    )
    slot_count = code.shape[1] // reply.shape[0]
    update = run_place(code, reply, field, slot_count, comps)
    return update.transpose(0, 2, 1, 3)[None]


def solution(mesh):
    placed = (
        P("grid", "px", "py", None, None),
        P("grid", "px", "py", None, None),
        P("grid", "px", "py", None, None),
        P("grid", "px", "py", None),
        P("grid", "px", "py", None, None),
        P("grid", "px", "py", None, None),
        P("grid", "px", "py", None, None),
    )
    return jax.shard_map(
        local,
        mesh=mesh,
        in_specs=placed,
        out_specs=P("grid", "px", "py", None, None),
        check_vma=False,
    )
```

time: 139 us -> 80.6 us (0.58)
  Pallas kernels: 93.7 us -> 74.6 us
  local copies, waits for them, and re-layouts: 21.4 us -> 5.6 us
  blocking collectives: 9.91 us -> 0 us
  starting transfers between devices: 8.73 us -> 0 us
  waiting for transfers between devices: 2.99 us -> 0 us
  other arithmetic: 1.71 us -> 0 us
    pallas_call x4 -> x2, Pallas kernels: 93.7 us -> 74.6 us  [the longest x1 69.7 us: run_sweeps(): pl.pallas_call(functools.partial(sweep_kernel, dims), out_shape=(jax.Shap...]
    unnamed x16 -> x12, local copies, waits for them, and re-layouts: 16.6 us -> 5.6 us
    all_to_all x1 -> x0, blocking collectives: 9.91 us -> none  [local(): lax.all_to_all(values, ('px', 'py'), split_axis=0, concat_axis=0, tiled=T...]
    all_to_all x1 -> x0, starting transfers between devices: 8.22 us -> none  [local(): lax.all_to_all(packet, ('px', 'py'), split_axis=0, concat_axis=0, tiled=T...]
    reshape x7 -> x0, local copies, waits for them, and re-layouts: 4.08 us -> none  [the longest x1 1.84 us: local(): return update.reshape(1, ci, cj, comps, length)]
    ppermute x2 -> x0, waiting for transfers between devices: 2.99 us -> none  [swapped(): lax.ppermute(array, axis, [(i, i ^ 1 << distance) for i in range(lax.axis...]
    all_to_all x2 -> x0, other arithmetic: 1.68 us -> none  [the longest x1 0.97 us: local(): lax.all_to_all(packet, ('px', 'py'), split_axis=0, concat_axis=0, tiled=T...]
  transfers between devices with their start and end apart: 3 -> 0, of which waited for: 2 -> 0; matrix products, arithmetic and copies ran while one was open for 9% -> 0% of each run, Pallas kernels for 45% -> 0%
where the time goes in v1:
time: 80.6 us; the launch traced here: 80.2 us
  Pallas kernels  74.6 us (93%)
  local copies, waits for them, and re-layouts  5.6 us (7%)
    pallas_call x1, Pallas kernels, run_sweeps(): pl.pallas_call(functools.partial(sweep_kernel, dims), out_shape=(jax.Shap...  69.7 us
    unnamed x12, local copies, waits for them, and re-layouts  5.6 us
    pallas_call x1, Pallas kernels, run_place(): pl.pallas_call(functools.partial(place_kernel, (ci, cj, comps, blocks, sl...  4.91 us

profile of v1, /device:TPU:0, one launch (start us, length us, event | category | flops | bytes accessed | tf_op | source)
XLA Modules:
  0.0 80.2 jit_solution(12942335372406667532)
XLA Ops:
  0.0 0.0 copy-start.1
  0.0 1.2 %copy-done.1 = f32[1,8,8,4,1024]{4,3,2,1,0:T(4,128)S(1)} copy-done((f32[1,8,8,4,1024]{4,3,2,1,0:T(4,128)S(1)}, f32[1,8,8,4,1024]{4,3,2,1,0:T(4,128)}, u32[]{:S(2)}) %copy-start.1) | copy-done | bytes 1048600
  1.2 0.0 copy-start.2
  1.2 0.7 copy-done.2
  1.9 0.0 copy-start.3
  1.9 0.7 copy-done.3
  2.7 0.0 copy-start.4
  2.7 0.7 copy-done.4
  3.3 0.0 copy-start.5
  3.3 0.7 copy-done.5
  4.0 69.7 %shard_map.73 = (f32[8,8,8,8,128]{4,3,2,1,0:T(8,128)}, s32[1,1024]{1,0:T(1,128)S(1)}, f32[16,8,128]{2,1,0:T(8,128)S(1)}) custom-call(f32[8,5,8,1024]{3,2,1,0:T(8,128)} %bitcast.24, f32[8,25,8,1024]{3,2,1,0:T(8,128)} %bitcast.23, f32[8,8,4,1024]{3,2,1,0:T(4,128)S(1)} %bitcast.18, s32[1,512]{1,0:T(1,128)S(1)} %bitcast.21, s32[8,512]{1,0:T(8,128)S(1)} %bitcast.19, ...), custom_call_target="tpu_custom_call" | custom-call | tf_op jit(solution)/shard_map/pallas_call | solution.py:494
  73.7 0.0 copy-start
  73.7 1.6 %copy-done = f32[8,8,8,8,128]{4,3,2,1,0:T(8,128)S(1)} copy-done((f32[8,8,8,8,128]{4,3,2,1,0:T(8,128)S(1)}, f32[8,8,8,8,128]{4,3,2,1,0:T(8,128)}, u32[]{:S(2)}) %copy-start) | copy-done | bytes 2097176
  75.3 4.9 %shard_map.74 = f32[8,5,8,1024]{3,2,1,0:T(8,128)} custom-call(s32[1,1024]{1,0:T(1,128)S(1)} %get-tuple-element.8.code, f32[16,8,128]{2,1,0:T(8,128)S(1)} %get-tuple-element.9.reply, f32[8,8,8,8,128]{4,3,2,1,0:T(8,128)S(1)} %copy-done), custom_call_target="tpu_custom_call" | custom-call | tf_op jit(solution)/shard_map/pallas_call | solution.py:564
Async XLA Ops:
  0.0 1.2 %copy-start.1 = (f32[1,8,8,4,1024]{4,3,2,1,0:T(4,128)S(1)}, f32[1,8,8,4,1024]{4,3,2,1,0:T(4,128)}, u32[]{:S(2)}) copy-start(f32[1,8,8,4,1024]{4,3,2,1,0:T(4,128)} %param.9) | copy-start | bytes 3145732
  1.2 0.7 copy-start.2
  1.9 0.7 copy-start.3
  2.7 0.7 copy-start.4
  3.3 0.7 copy-start.5
  73.7 1.6 %copy-start = (f32[8,8,8,8,128]{4,3,2,1,0:T(8,128)S(1)}, f32[8,8,8,8,128]{4,3,2,1,0:T(8,128)}, u32[]{:S(2)}) copy-start(f32[8,8,8,8,128]{4,3,2,1,0:T(8,128)} %get-tuple-element.10.field) | copy-start | bytes 6291460

commit v2 on v1

--- a/solution.py
+++ b/solution.py
@@ -25,18 +25,21 @@
     res_hbm,
     inv_hbm,
     cpl_hbm,
+    owners_hbm,
+    donors_hbm,
+    weights_hbm,
+    receptors_hbm,
+    field_v,
+    code_out,
+    reply_out,
     owners,
     donors,
     weights,
     receptors,
-    out_hbm,
-    code_out,
-    reply_out,
     inv_v,
     res_v,
     cpl_v,
     star_v,
-    field_v,
     face_send,
     face_recv,
     ask_send,
@@ -47,7 +50,7 @@
     reply_send,
     reply_recv,
     in_sem,
-    out_sem,
+    small_sem,
     send_sem,
     recv_sem,
     ask_send_sem,
@@ -88,9 +91,22 @@
             ),
         )
 
+    small_copies = [
+        pltpu.make_async_copy(source, target, small_sem.at[t])
+        for t, (source, target) in enumerate(
+            (
+                (owners_hbm, owners),
+                (donors_hbm, donors),
+                (weights_hbm, weights),
+                (receptors_hbm, receptors),
+            )
+        )
+    ]
     for kb in range(blocks):
         for copy in input_copies(kb):
             copy.start()
+    for copy in small_copies:
+        copy.start()
 
     has_prev_row = px > 0
     has_next_row = px < count_rows - 1
@@ -169,6 +185,8 @@
         return [(value >> LOW).astype(jnp.float32), (value & (2**LOW - 1)).astype(jnp.float32)]
 
     def plan():
+        for copy in small_copies:
+            copy.wait()
         owner = owners[...]
         ones = jnp.where(
             owner == lax.broadcasted_iota(jnp.int32, (owner_count, count), 0), 1.0, 0.0
@@ -208,7 +226,7 @@
             target = (mark[0:1] * float(2**LOW) + mark[1:2]).astype(jnp.int32)
             pencil, k = divmod_const(target, length)
             kb, spot = divmod_const(k, LANES)
-            line = kb * (ci * cj) + pencil
+            line = kb * (tall * cj) + (cj - 1) * cj + pencil
             code_out[:, base : base + wide] = jnp.where(
                 mark[2:3] > 0.5, line * (2 * LANES) + spot, EMPTY
             )
@@ -362,11 +380,6 @@
         start_send(0, kb)
         start_send(1, kb)
 
-    def out_copy(kb):
-        return pltpu.make_async_copy(
-            field_v.at[kb, pl.ds(cj - 1, ci)], out_hbm.at[kb], out_sem.at[kb]
-        )
-
     def backward(kb):
         wait_recv(2, kb)
         wait_recv(3, kb)
@@ -406,7 +419,6 @@
             face_send[2, kb, pl.ds(c * ROWS, cj), :] = upper[c]
         start_send(2, kb)
         start_send(3, kb)
-        out_copy(kb).start()
 
     middle = blocks + 1
     last = 2 * blocks + 2
@@ -432,27 +444,21 @@
             prepare()
 
     lane8 = lax.broadcasted_iota(jnp.int32, (ROWS, LANES), 1)
-    turn = min(16, slot_count)
 
     @pl.loop(0, owner_count)
     def _(q):
-        def body(t, acc):
-            for u in range(turn):
-                s = t * turn + u
-                parts = [
-                    field_rows[rows_s[q * ROWS + d, s]]
-                    * spread[d, pl.ds(q * slot_count + s, 1), :]
-                    for d in range(many)
-                ]
-                while len(parts) > 1:
-                    parts = [parts[i] + parts[i + 1] for i in range(0, len(parts), 2)]
-                total = jnp.sum(parts[0], axis=1, keepdims=True)
-                acc = jnp.where(lane8 == s, total, acc)
-            return acc
-
-        reply_send[q] = lax.fori_loop(
-            0, slot_count // turn, body, jnp.zeros((ROWS, LANES), jnp.float32)
-        )
+        acc = jnp.zeros((ROWS, LANES), jnp.float32)
+        for s in range(slot_count):
+            parts = [
+                field_rows[rows_s[q * ROWS + d, s]]
+                * spread[d, pl.ds(q * slot_count + s, 1), :]
+                for d in range(many)
+            ]
+            while len(parts) > 1:
+                parts = [parts[i] + parts[i + 1] for i in range(0, len(parts), 2)]
+            total = jnp.sum(parts[0], axis=1, keepdims=True)
+            acc = jnp.where(lane8 == s, total, acc)
+        reply_send[q] = acc
         reply(q).start()
 
     @pl.loop(0, owner_count)
@@ -466,7 +472,6 @@
         reply(q).wait_send()
 
     for kb in range(blocks):
-        out_copy(kb).wait()
         for kind in range(4):
 
             @pl.when(puts[kind])
@@ -475,6 +480,7 @@
 
 
 def run_sweeps(residual, inverses, couplings, owners, donors, weights, receptors):
+    inputs = (residual, inverses, couplings, owners, donors, weights, receptors)
     ci, comps, cj, length = residual.shape
     many, count = donors.shape
     blocks = length // LANES
@@ -489,23 +495,26 @@
     dims = (ci, cj, comps, blocks, rows, cols, slot_count)
     face = comps * ROWS
     dma = pltpu.SemaphoreType.DMA
-    hbm = pl.BlockSpec(memory_space=pl.ANY)
+    hbm = pl.BlockSpec(memory_space=pltpu.HBM)
     vmem = pl.BlockSpec(memory_space=pltpu.VMEM)
     return pl.pallas_call(
         functools.partial(sweep_kernel, dims),
         out_shape=(
-            jax.ShapeDtypeStruct((blocks, ci, cj, ROWS, LANES), jnp.float32),
-            jax.ShapeDtypeStruct((1, slots), jnp.int32),
-            jax.ShapeDtypeStruct((owner_count, ROWS, LANES), jnp.float32),
+            pltpu.VMEM((blocks, tall, cj, ROWS, LANES), jnp.float32),
+            pltpu.VMEM((1, slots), jnp.int32),
+            pltpu.VMEM((owner_count, ROWS, LANES), jnp.float32),
         ),
-        in_specs=[hbm] * 3 + [vmem] * 4,
-        out_specs=(hbm, vmem, vmem),
+        in_specs=[hbm] * 7,
+        out_specs=(vmem, vmem, vmem),
         scratch_shapes=[
+            pltpu.VMEM(owners.shape, owners.dtype),
+            pltpu.VMEM(donors.shape, donors.dtype),
+            pltpu.VMEM(weights.shape, weights.dtype),
+            pltpu.VMEM(receptors.shape, receptors.dtype),
             pltpu.VMEM((blocks, tall, comps * comps, cj, LANES), jnp.float32),
             pltpu.VMEM((blocks, tall, comps, cj, LANES), jnp.float32),
             pltpu.VMEM((blocks, tall, cj, ROWS, LANES), jnp.float32),
             pltpu.VMEM((blocks, steps, comps, cj, LANES), jnp.float32),
-            pltpu.VMEM((blocks, tall, cj, ROWS, LANES), jnp.float32),
             pltpu.VMEM((4, blocks, face, LANES), jnp.float32),
             pltpu.VMEM((4, blocks, face, LANES), jnp.float32),
             pltpu.VMEM((owner_count, ROWS, LANES), jnp.float32),
@@ -516,7 +525,7 @@
             pltpu.VMEM((owner_count, ROWS, LANES), jnp.float32),
             pltpu.VMEM((owner_count, ROWS, LANES), jnp.float32),
             dma((3, blocks)),
-            dma((blocks,)),
+            dma((4,)),
             dma((4, blocks)),
             dma((4, blocks)),
             dma((owner_count,)),
@@ -526,19 +535,17 @@
             dma,
         ],
         compiler_params=pltpu.CompilerParams(
-            collective_id=0, has_side_effects=True, vmem_limit_bytes=52 * 1024 * 1024
+            collective_id=0, has_side_effects=True, vmem_limit_bytes=40 * 1024 * 1024
         ),
-    )(residual, inverses, couplings, owners, donors, weights, receptors)
-
-
-def place_kernel(dims, code, reply, field, out, work, sem):
-    ci, cj, comps, blocks, slot_count = dims
+    )(*(pltpu.with_memory_space_constraint(x, pltpu.HBM) for x in inputs))
+
+
+def place_kernel(dims, code, reply, field, out, work):
+    ci, cj, comps, slot_count = dims
     owner_count = reply.shape[0]
-    copy = pltpu.make_async_copy(field, work, sem)
-    copy.start()
-    copy.wait()
+    blocks, tall = field.shape[:2]
     lane = lax.broadcasted_iota(jnp.int32, (ROWS, LANES), 1)
-    lines = work.reshape(blocks * ci * cj, ROWS, LANES)
+    lines = work.reshape(blocks * tall * cj, ROWS, LANES)
 
     @pl.loop(0, owner_count)
     def _(q):
@@ -548,38 +555,36 @@
             value = jnp.broadcast_to(tile[:, s : s + 1], (ROWS, LANES))
             pltpu.store(lines.at[line], value, mask=lane == spot)
 
-    stack = work.reshape(blocks, ci, cj * ROWS, LANES)
+    stack = work.reshape(blocks, tall, cj * ROWS, LANES)
 
     @pl.loop(0, ci)
     def _(i):
         for kb in range(blocks):
             for c in range(comps):
                 out[i, c, :, kb * LANES : (kb + 1) * LANES] = stack[
-                    kb, i, pl.ds(c, cj, stride=ROWS), :
+                    kb, i + cj - 1, pl.ds(c, cj, stride=ROWS), :
                 ]
 
 
-def run_place(code, reply, field, slot_count, comps):
-    blocks, ci, cj = field.shape[:3]
+def run_place(code, reply, field, dims):
+    ci, cj, comps, slot_count = dims
+    blocks = field.shape[0]
+    vmem = pl.BlockSpec(memory_space=pltpu.VMEM)
     return pl.pallas_call(
-        functools.partial(place_kernel, (ci, cj, comps, blocks, slot_count)),
-        out_shape=jax.ShapeDtypeStruct((ci, comps, cj, blocks * LANES), jnp.float32),
-        in_specs=[
-            pl.BlockSpec(memory_space=pltpu.SMEM),
-            pl.BlockSpec(memory_space=pltpu.VMEM),
-            pl.BlockSpec(memory_space=pl.ANY),
-        ],
-        out_specs=pl.BlockSpec(memory_space=pltpu.VMEM),
-        scratch_shapes=[
-            pltpu.VMEM(field.shape, jnp.float32),
-            pltpu.SemaphoreType.DMA,
-        ],
+        functools.partial(place_kernel, dims),
+        out_shape=(
+            jax.ShapeDtypeStruct((ci, comps, cj, blocks * LANES), jnp.float32),
+            jax.ShapeDtypeStruct(field.shape, jnp.float32),
+        ),
+        in_specs=[pl.BlockSpec(memory_space=pltpu.SMEM), vmem, vmem],
+        out_specs=(vmem, vmem),
+        input_output_aliases={2: 1},
         compiler_params=pltpu.CompilerParams(vmem_limit_bytes=16 * 1024 * 1024),
-    )(code, reply, field)
+    )(code, reply, field)[0]
 
 
 def local(residual, inverses, couplings, receptors, owners, donors, weights):
-    comps = residual.shape[3]
+    ci, cj, comps = residual.shape[1:4]
     many = donors.shape[-1]
     count = donors.shape[-2]
     field, code, reply = run_sweeps(
@@ -592,7 +597,7 @@
         receptors.reshape(1, count),
     )
     slot_count = code.shape[1] // reply.shape[0]
-    update = run_place(code, reply, field, slot_count, comps)
+    update = run_place(code, reply, field, (ci, cj, comps, slot_count))
     return update.transpose(0, 2, 1, 3)[None]
 
 

time: 80.6 us -> 66 us (0.82)
  Pallas kernels: 74.6 us -> 65.9 us
  local copies, waits for them, and re-layouts: 5.6 us -> 0 us
    pallas_call x2, Pallas kernels: 74.6 us -> 65.9 us  [the longest x1 61.1 us: run_sweeps(): pl.pallas_call(functools.partial(sweep_kernel, dims), out_shape=(pltpu.VM...]
    unnamed x12 -> x0, local copies, waits for them, and re-layouts: 5.6 us -> none
where the time goes in v2:
time: 66 us; the launch traced here: 65.9 us
  Pallas kernels  65.9 us (100%)
    pallas_call x1, Pallas kernels, run_sweeps(): pl.pallas_call(functools.partial(sweep_kernel, dims), out_shape=(pltpu.VM...  61.1 us
    pallas_call x1, Pallas kernels, run_place(): pl.pallas_call(functools.partial(place_kernel, dims), out_shape=(jax.Shap...  4.76 us

profile of v2, /device:TPU:0, one launch (start us, length us, event | category | flops | bytes accessed | tf_op | source)
XLA Modules:
  0.0 65.9 jit_solution(2120090958303308024)
XLA Ops:
  0.0 61.1 %shard_map.73 = (f32[8,22,8,8,128]{4,3,2,1,0:T(8,128)S(1)}, s32[1,1024]{1,0:T(1,128)S(1)}, f32[16,8,128]{2,1,0:T(8,128)S(1)}) custom-call(f32[8,5,8,1024]{3,2,1,0:T(8,128)} %bitcast.19, f32[8,25,8,1024]{3,2,1,0:T(8,128)} %bitcast.18, f32[8,8,4,1024]{3,2,1,0:T(4,128)} %bitcast.20, s32[1,512]{1,0:T(1,128)} %bitcast.23, s32[8,512]{1,0:T(8,128)} %bitcast.21, ...), custom_call_target="tpu_custom_call" | custom-call | tf_op jit(solution)/shard_map/pallas_call | solution.py:500
  61.1 4.8 %shard_map.74 = (f32[8,5,8,1024]{3,2,1,0:T(8,128)}, f32[8,22,8,8,128]{4,3,2,1,0:T(8,128)S(1)}) custom-call(s32[1,1024]{1,0:T(1,128)S(1)} %get-tuple-element.9.code, f32[16,8,128]{2,1,0:T(8,128)S(1)} %get-tuple-element.10.reply, f32[8,22,8,8,128]{4,3,2,1,0:T(8,128)S(1)} %get-tuple-element.11.field), custom_call_target="tpu_custom_call", output_to_operand_aliasing={{1}: (2, {})} | custom-call | tf_op jit(solution)/shard_map/pallas_call | solution.py:573

commit v3 on v2

--- a/solution.py
+++ b/solution.py
@@ -58,6 +58,7 @@
     reply_send_sem,
     reply_recv_sem,
     rows_sem,
+    wave_sem,
 ):
     ci, cj, comps, blocks, count_rows, count_cols, slot_count = dims
     length = blocks * LANES
@@ -102,7 +103,8 @@
             )
         )
     ]
-    for kb in range(blocks):
+    eager = min(2, blocks)
+    for kb in range(eager):
         for copy in input_copies(kb):
             copy.start()
     for copy in small_copies:
@@ -133,13 +135,40 @@
         def _():
             pl.semaphore_signal(barrier, inc=1, device_id=device, device_id_type=MESH)
 
-    @pl.loop(0, owner_count)
-    def _(q):
-        pl.semaphore_signal(barrier, inc=1, device_id=other(q), device_id_type=MESH)
+    pl.semaphore_signal(
+        barrier, inc=1, device_id={"grid": 1 - grid}, device_id_type=MESH
+    )
 
     def enter():
         near = sum(there.astype(jnp.int32) for there, _ in sides)
-        pl.semaphore_wait(barrier, near + owner_count)
+        pl.semaphore_wait(barrier, near + 1)
+
+    def wave(came_from, goes_to):
+        for kind, there, _ in came_from:
+
+            @pl.when(there)
+            def _():
+                pl.semaphore_wait(wave_sem.at[kind], 1)
+
+        for kind, there, device in goes_to:
+
+            @pl.when(there)
+            def _():
+                pl.semaphore_signal(
+                    wave_sem.at[kind], inc=1, device_id=device, device_id_type=MESH
+                )
+
+    def wave_on():
+        wave(
+            ((0, has_prev_row, prev_row), (1, has_prev_col, prev_col)),
+            ((0, has_next_row, next_row), (1, has_next_col, next_col)),
+        )
+
+    def wave_back():
+        wave(
+            ((2, has_next_row, next_row), (3, has_next_col, next_col)),
+            ((2, has_prev_row, prev_row), (3, has_prev_col, prev_col)),
+        )
 
     def ask(q):
         return pltpu.make_async_remote_copy(
@@ -242,9 +271,8 @@
                     right = pltpu.roll(right, (slot_count - shift) % LANES, 1)
                 ask_send[q] = jnp.where(lane < slot_count, left, right)
 
-        @pl.when(ahead >= 2)
-        def _():
-            enter()
+    def send_asks():
+        wave_back()
 
         @pl.loop(0, owner_count)
         def _(q):
@@ -272,9 +300,12 @@
                 share = turned[slot_count : 2 * slot_count, d : d + 1]
                 spread[d, pl.ds(first, slot_count), :] = jnp.where(line == spot, share, 0.0)
 
-        copy = pltpu.make_async_copy(rows_v, rows_s, rows_sem)
-        copy.start()
-        copy.wait()
+    def fetch_rows(q, slot):
+        return pltpu.make_async_copy(
+            rows_v.at[pl.ds(pl.multiple_of(q * ROWS, ROWS), ROWS)],
+            rows_s.at[slot],
+            rows_sem.at[slot],
+        )
 
     def send(kind, kb):
         device = (next_row, next_col, prev_row, prev_col)[kind]
@@ -287,6 +318,7 @@
             device_id_type=MESH,
         )
 
+    idle_first = ahead >= 2
     gets = (has_prev_row, has_prev_col, has_next_row, has_next_col)
     puts = (has_next_row, has_next_col, has_prev_row, has_prev_col)
 
@@ -336,6 +368,13 @@
     def forward(kb):
         for copy in input_copies(kb):
             copy.wait()
+
+        @pl.when(kb == 0)
+        def _():
+            for later in range(eager, blocks):
+                for copy in input_copies(later):
+                    copy.start()
+
         wait_recv(0, kb)
         wait_recv(1, kb)
         upper = [face_recv[0, kb, pl.ds(c * ROWS, cj), :] for c in range(comps)]
@@ -373,12 +412,16 @@
         for c in range(comps):
             face_send[0, kb, pl.ds(c * ROWS, cj), :] = lower[c]
 
-        @pl.when((kb == 0) & (ahead < 2))
+        @pl.when((kb == 0) & jnp.logical_not(idle_first))
         def _():
             enter()
 
         start_send(0, kb)
         start_send(1, kb)
+
+        @pl.when((kb == 0) & jnp.logical_not(idle_first))
+        def _():
+            wave_on()
 
     def backward(kb):
         wait_recv(2, kb)
@@ -423,14 +466,24 @@
     middle = blocks + 1
     last = 2 * blocks + 2
     begin = jnp.where(ahead == reach, 1, blocks + 2)
-    early = ahead + 2 <= reach
+    early = ahead + 3 <= reach
+    asks_first = ahead * 3 >= reach * 2
 
     @pl.loop(0, last + 1)
     def _(n):
-        @pl.when(((n == 0) & (ahead >= 2)) | ((n == middle) & (ahead < 2)))
+        @pl.when((n == 0) & idle_first)
+        def _():
+            enter()
+            wave_on()
+
+        @pl.when(((n == 0) & idle_first) | ((n == middle) & jnp.logical_not(idle_first)))
         def _():
             plan()
 
+        @pl.when(((n == 0) & asks_first) | ((n == middle) & jnp.logical_not(asks_first)))
+        def _():
+            send_asks()
+
         @pl.when((n >= 1) & (n <= blocks))
         def _():
             forward(n - 1)
@@ -445,13 +498,11 @@
 
     lane8 = lax.broadcasted_iota(jnp.int32, (ROWS, LANES), 1)
 
-    @pl.loop(0, owner_count)
-    def _(q):
+    def gather(q, slot):
         acc = jnp.zeros((ROWS, LANES), jnp.float32)
         for s in range(slot_count):
             parts = [
-                field_rows[rows_s[q * ROWS + d, s]]
-                * spread[d, pl.ds(q * slot_count + s, 1), :]
+                field_rows[rows_s[slot, d, s]] * spread[d, pl.ds(q * slot_count + s, 1), :]
                 for d in range(many)
             ]
             while len(parts) > 1:
@@ -460,6 +511,22 @@
             acc = jnp.where(lane8 == s, total, acc)
         reply_send[q] = acc
         reply(q).start()
+
+    fetch_rows(0, 0).start()
+
+    @pl.loop(0, owner_count // 2)
+    def _(pair):
+        q = 2 * pair
+        fetch_rows(q + 1, 1).start()
+        fetch_rows(q, 0).wait()
+        gather(q, 0)
+
+        @pl.when(pair + 1 < owner_count // 2)
+        def _():
+            fetch_rows(q + 2, 0).start()
+
+        fetch_rows(q + 1, 1).wait()
+        gather(q + 1, 1)
 
     @pl.loop(0, owner_count)
     def _(q):
@@ -490,7 +557,7 @@
     owner_count = rows * cols
     slot_count = max(2, 2 * count // owner_count)
     slots = owner_count * slot_count
-    assert cj == ROWS and ci <= ROWS and many == ROWS and 2 * slot_count <= LANES
+    assert owner_count % 2 == 0 and cj == ROWS and ci <= ROWS and many == ROWS and 2 * slot_count <= LANES
     assert ci * cj * length <= 2 ** (2 * LOW)
     dims = (ci, cj, comps, blocks, rows, cols, slot_count)
     face = comps * ROWS
@@ -520,7 +587,7 @@
             pltpu.VMEM((owner_count, ROWS, LANES), jnp.float32),
             pltpu.VMEM((owner_count, ROWS, LANES), jnp.float32),
             pltpu.VMEM((owner_count * ROWS, LANES), jnp.int32),
-            pltpu.SMEM((owner_count * ROWS, LANES), jnp.int32),
+            pltpu.SMEM((2, ROWS, LANES), jnp.int32),
             pltpu.VMEM((many, slots, LANES), jnp.float32),
             pltpu.VMEM((owner_count, ROWS, LANES), jnp.float32),
             pltpu.VMEM((owner_count, ROWS, LANES), jnp.float32),
@@ -532,7 +599,8 @@
             dma((owner_count,)),
             dma((owner_count,)),
             dma((owner_count,)),
-            dma,
+            dma((2,)),
+            pltpu.SemaphoreType.REGULAR((4,)),
         ],
         compiler_params=pltpu.CompilerParams(
             collective_id=0, has_side_effects=True, vmem_limit_bytes=40 * 1024 * 1024

time: 66 us -> 61.4 us (0.930)
  Pallas kernels: 65.9 us -> 61.2 us
    pallas_call x1, Pallas kernels: 61.1 us -> 56.4 us  [run_sweeps(): pl.pallas_call(functools.partial(sweep_kernel, dims), out_shape=(pltpu.VM...]
where the time goes in v3:
time: 61.4 us; the launch traced here: 61.2 us
  Pallas kernels  61.2 us (100%)
    pallas_call x1, Pallas kernels, run_sweeps(): pl.pallas_call(functools.partial(sweep_kernel, dims), out_shape=(pltpu.VM...  56.4 us
    pallas_call x1, Pallas kernels, run_place(): pl.pallas_call(functools.partial(place_kernel, dims), out_shape=(jax.Shap...  4.76 us

profile of v3, /device:TPU:0, one launch (start us, length us, event | category | flops | bytes accessed | tf_op | source)
XLA Modules:
  0.0 61.2 jit_solution(14898397759154734398)
XLA Ops:
  0.0 56.4 %shard_map.73 = (f32[8,22,8,8,128]{4,3,2,1,0:T(8,128)S(1)}, s32[1,1024]{1,0:T(1,128)S(1)}, f32[16,8,128]{2,1,0:T(8,128)S(1)}) custom-call(f32[8,5,8,1024]{3,2,1,0:T(8,128)} %bitcast.19, f32[8,25,8,1024]{3,2,1,0:T(8,128)} %bitcast.18, f32[8,8,4,1024]{3,2,1,0:T(4,128)} %bitcast.20, s32[1,512]{1,0:T(1,128)} %bitcast.23, s32[8,512]{1,0:T(8,128)} %bitcast.21, ...), custom_call_target="tpu_custom_call" | custom-call | tf_op jit(solution)/shard_map/pallas_call | solution.py:567
  56.5 4.8 %shard_map.74 = (f32[8,5,8,1024]{3,2,1,0:T(8,128)}, f32[8,22,8,8,128]{4,3,2,1,0:T(8,128)S(1)}) custom-call(s32[1,1024]{1,0:T(1,128)S(1)} %get-tuple-element.9.code, f32[16,8,128]{2,1,0:T(8,128)S(1)} %get-tuple-element.10.reply, f32[8,22,8,8,128]{4,3,2,1,0:T(8,128)S(1)} %get-tuple-element.11.field), custom_call_target="tpu_custom_call", output_to_operand_aliasing={{1}: (2, {})} | custom-call | tf_op jit(solution)/shard_map/pallas_call | solution.py:641

commit v4 on v3

--- a/solution.py
+++ b/solution.py
@@ -12,6 +12,7 @@
 ROWS = 8
 LOW = 8
 EMPTY = LANES
+FETCHES = 4
 
 
 def divmod_const(value, by):
@@ -318,6 +319,7 @@
             device_id_type=MESH,
         )
 
+    wave_first = ahead >= 1
     idle_first = ahead >= 2
     gets = (has_prev_row, has_prev_col, has_next_row, has_next_col)
     puts = (has_next_row, has_next_col, has_prev_row, has_prev_col)
@@ -412,14 +414,14 @@
         for c in range(comps):
             face_send[0, kb, pl.ds(c * ROWS, cj), :] = lower[c]
 
-        @pl.when((kb == 0) & jnp.logical_not(idle_first))
+        @pl.when((kb == 0) & jnp.logical_not(wave_first))
         def _():
             enter()
 
         start_send(0, kb)
         start_send(1, kb)
 
-        @pl.when((kb == 0) & jnp.logical_not(idle_first))
+        @pl.when((kb == 0) & jnp.logical_not(wave_first))
         def _():
             wave_on()
 
@@ -466,12 +468,12 @@
     middle = blocks + 1
     last = 2 * blocks + 2
     begin = jnp.where(ahead == reach, 1, blocks + 2)
-    early = ahead + 3 <= reach
+    early = ahead * 3 <= reach
     asks_first = ahead * 3 >= reach * 2
 
     @pl.loop(0, last + 1)
     def _(n):
-        @pl.when((n == 0) & idle_first)
+        @pl.when((n == 0) & wave_first)
         def _():
             enter()
             wave_on()
@@ -512,21 +514,21 @@
         reply_send[q] = acc
         reply(q).start()
 
-    fetch_rows(0, 0).start()
-
-    @pl.loop(0, owner_count // 2)
-    def _(pair):
-        q = 2 * pair
-        fetch_rows(q + 1, 1).start()
-        fetch_rows(q, 0).wait()
-        gather(q, 0)
-
-        @pl.when(pair + 1 < owner_count // 2)
-        def _():
-            fetch_rows(q + 2, 0).start()
-
-        fetch_rows(q + 1, 1).wait()
-        gather(q + 1, 1)
+    for slot in range(FETCHES - 1):
+        fetch_rows(slot, slot).start()
+
+    @pl.loop(0, owner_count // FETCHES)
+    def _(turn):
+        for slot in range(FETCHES):
+            q = turn * FETCHES + slot
+            following = q + FETCHES - 1
+
+            @pl.when(following < owner_count)
+            def _():
+                fetch_rows(following, (slot + FETCHES - 1) % FETCHES).start()
+
+            fetch_rows(q, slot).wait()
+            gather(q, slot)
 
     @pl.loop(0, owner_count)
     def _(q):
@@ -557,7 +559,7 @@
     owner_count = rows * cols
     slot_count = max(2, 2 * count // owner_count)
     slots = owner_count * slot_count
-    assert owner_count % 2 == 0 and cj == ROWS and ci <= ROWS and many == ROWS and 2 * slot_count <= LANES
+    assert owner_count % FETCHES == 0 and cj == ROWS and ci <= ROWS and many == ROWS and 2 * slot_count <= LANES
     assert ci * cj * length <= 2 ** (2 * LOW)
     dims = (ci, cj, comps, blocks, rows, cols, slot_count)
     face = comps * ROWS
@@ -587,7 +589,7 @@
             pltpu.VMEM((owner_count, ROWS, LANES), jnp.float32),
             pltpu.VMEM((owner_count, ROWS, LANES), jnp.float32),
             pltpu.VMEM((owner_count * ROWS, LANES), jnp.int32),
-            pltpu.SMEM((2, ROWS, LANES), jnp.int32),
+            pltpu.SMEM((FETCHES, ROWS, LANES), jnp.int32),
             pltpu.VMEM((many, slots, LANES), jnp.float32),
             pltpu.VMEM((owner_count, ROWS, LANES), jnp.float32),
             pltpu.VMEM((owner_count, ROWS, LANES), jnp.float32),
@@ -599,7 +601,7 @@
             dma((owner_count,)),
             dma((owner_count,)),
             dma((owner_count,)),
-            dma((2,)),
+            dma((FETCHES,)),
             pltpu.SemaphoreType.REGULAR((4,)),
         ],
         compiler_params=pltpu.CompilerParams(

time: 61.4 us -> 60.8 us (level)
  no operation moved by 1% of the time
where the time goes in v4:
time: 60.8 us
  Pallas kernels  60.8 us (100%)
    pallas_call x1, Pallas kernels, run_sweeps(): pl.pallas_call(functools.partial(sweep_kernel, dims), out_shape=(pltpu.VM...  56 us
    pallas_call x1, Pallas kernels, run_place(): pl.pallas_call(functools.partial(place_kernel, dims), out_shape=(jax.Shap...  4.76 us

profile of v4, /device:TPU:0, one launch (start us, length us, event | category | flops | bytes accessed | tf_op | source)
XLA Modules:
  0.0 60.8 jit_solution(9741177737583433199)
XLA Ops:
  0.0 56.0 %shard_map.73 = (f32[8,22,8,8,128]{4,3,2,1,0:T(8,128)S(1)}, s32[1,1024]{1,0:T(1,128)S(1)}, f32[16,8,128]{2,1,0:T(8,128)S(1)}) custom-call(f32[8,5,8,1024]{3,2,1,0:T(8,128)} %bitcast.19, f32[8,25,8,1024]{3,2,1,0:T(8,128)} %bitcast.18, f32[8,8,4,1024]{3,2,1,0:T(4,128)} %bitcast.20, s32[1,512]{1,0:T(1,128)} %bitcast.23, s32[8,512]{1,0:T(8,128)} %bitcast.21, ...), custom_call_target="tpu_custom_call" | custom-call | tf_op jit(solution)/shard_map/pallas_call | solution.py:569
  56.0 4.8 %shard_map.74 = (f32[8,5,8,1024]{3,2,1,0:T(8,128)}, f32[8,22,8,8,128]{4,3,2,1,0:T(8,128)S(1)}) custom-call(s32[1,1024]{1,0:T(1,128)S(1)} %get-tuple-element.9.code, f32[16,8,128]{2,1,0:T(8,128)S(1)} %get-tuple-element.10.reply, f32[8,22,8,8,128]{4,3,2,1,0:T(8,128)S(1)} %get-tuple-element.11.field), custom_call_target="tpu_custom_call", output_to_operand_aliasing={{1}: (2, {})} | custom-call | tf_op jit(solution)/shard_map/pallas_call | solution.py:643

commit v5 on v4

--- a/solution.py
+++ b/solution.py
@@ -54,6 +54,8 @@
     small_sem,
     send_sem,
     recv_sem,
+    ship_send_sem,
+    ship_recv_sem,
     ask_send_sem,
     ask_recv_sem,
     reply_send_sem,
@@ -65,7 +67,7 @@
     length = blocks * LANES
     entries = comps * comps
     steps = ci + cj - 1
-    tall = ci + 2 * (cj - 1)
+    pitch = ci + cj - 1
     many, count = donors.shape
     owner_count = count_rows * count_cols
     slots = owner_count * slot_count
@@ -76,21 +78,54 @@
     ahead = px + py
     reach = count_rows + count_cols - 2
 
+    first_core = grid == 0
+    second_core = grid == 1
+
+    def is_far(at):
+        return at * 2 >= reach
+
+    def is_beyond(at):
+        return at >= 1
+
+    far = is_far(ahead)
+    beyond = is_beyond(ahead)
+    own_forward = second_core | jnp.logical_not(far)
+    own_backward = second_core | jnp.logical_not(beyond)
+    taken_forward = second_core & far
+    taken_backward = second_core & beyond
+
+    def rows_of(chunk):
+        return pl.ds(chunk * pitch + cj - 1, ci)
+
+    def inputs_of(kb, chunk):
+        lanes = pl.ds(pl.multiple_of(kb * LANES, LANES), LANES)
+        rows = rows_of(chunk)
+        return (
+            (inv_hbm.at[:, :, :, lanes], inv_v.at[rows]),
+            (cpl_hbm.at[:, :, :, lanes], cpl_v.at[rows, :, pl.ds(0, 4), :]),
+            (res_hbm.at[:, :, :, lanes], res_v.at[rows]),
+        )
+
     def input_copies(kb):
-        lanes = pl.ds(pl.multiple_of(kb * LANES, LANES), LANES)
-        mine = pl.ds(cj - 1, ci)
-        return (
-            pltpu.make_async_copy(
-                inv_hbm.at[:, :, :, lanes], inv_v.at[kb, mine], in_sem.at[0, kb]
-            ),
-            pltpu.make_async_copy(
-                res_hbm.at[:, :, :, lanes], res_v.at[kb, mine], in_sem.at[1, kb]
-            ),
-            pltpu.make_async_copy(
-                cpl_hbm.at[:, :, :, lanes],
-                cpl_v.at[kb, mine, :, pl.ds(0, 4), :],
-                in_sem.at[2, kb],
-            ),
+        return [
+            pltpu.make_async_copy(source, target, in_sem.at[t, kb])
+            for t, (source, target) in enumerate(inputs_of(kb, kb))
+        ]
+
+    def ship(kind, kb):
+        if kind < 3:
+            source, target = inputs_of(kb, blocks + kb)[kind]
+        elif kind == 3:
+            source, target = star_v.at[kb], star_v.at[blocks + kb]
+        else:
+            source, target = field_v.at[rows_of(blocks + kb)], field_v.at[rows_of(kb)]
+        return pltpu.make_async_remote_copy(
+            src_ref=source,
+            dst_ref=target,
+            send_sem=ship_send_sem.at[kind, kb],
+            recv_sem=ship_recv_sem.at[kind, kb],
+            device_id={"grid": 1 - grid},
+            device_id_type=MESH,
         )
 
     small_copies = [
@@ -105,9 +140,13 @@
         )
     ]
     eager = min(2, blocks)
-    for kb in range(eager):
-        for copy in input_copies(kb):
-            copy.start()
+
+    @pl.when(own_forward)
+    def _():
+        for kb in range(eager):
+            for copy in input_copies(kb):
+                copy.start()
+
     for copy in small_copies:
         copy.start()
 
@@ -134,7 +173,10 @@
 
         @pl.when(there)
         def _():
-            pl.semaphore_signal(barrier, inc=1, device_id=device, device_id_type=MESH)
+            for core in range(2):
+                pl.semaphore_signal(
+                    barrier, inc=1, device_id=dict(device, grid=core), device_id_type=MESH
+                )
 
     pl.semaphore_signal(
         barrier, inc=1, device_id={"grid": 1 - grid}, device_id_type=MESH
@@ -142,7 +184,7 @@
 
     def enter():
         near = sum(there.astype(jnp.int32) for there, _ in sides)
-        pl.semaphore_wait(barrier, near + 1)
+        pl.semaphore_wait(barrier, 2 * near + 1)
 
     def wave(came_from, goes_to):
         for kind, there, _ in came_from:
@@ -256,7 +298,7 @@
             target = (mark[0:1] * float(2**LOW) + mark[1:2]).astype(jnp.int32)
             pencil, k = divmod_const(target, length)
             kb, spot = divmod_const(k, LANES)
-            line = kb * (tall * cj) + (cj - 1) * cj + pencil
+            line = kb * (pitch * cj) + (cj - 1) * cj + pencil
             code_out[:, base : base + wide] = jnp.where(
                 mark[2:3] > 0.5, line * (2 * LANES) + spot, EMPTY
             )
@@ -290,9 +332,9 @@
             pencil, k = divmod_const(cell, length)
             kb, _ = divmod_const(k, LANES)
             i, j = divmod_const(pencil, cj)
-            row = kb * (tall * cj) + (i + (cj - 1)) * cj + j
+            row = kb * (pitch * cj) + (i + (cj - 1)) * cj + j
             rows_v[pl.ds(pl.multiple_of(q * ROWS, ROWS), ROWS), :] = jnp.clip(
-                row, 0, blocks * tall * cj - 1
+                row, 0, field_v.shape[0] * cj - 1
             )
             turned = tile.T
             first = pl.multiple_of(q * slot_count, slot_count)
@@ -308,14 +350,27 @@
             rows_sem.at[slot],
         )
 
-    def send(kind, kb):
+    def send(kind, chunk):
         device = (next_row, next_col, prev_row, prev_col)[kind]
+        taken = chunk >= blocks
+        moves = (first_core | taken) & (is_far(ahead + 1) if kind < 2 else is_beyond(ahead - 1))
+        target = chunk - jnp.where(taken, blocks, 0) + jnp.where(moves, blocks, 0)
         return pltpu.make_async_remote_copy(
-            src_ref=face_send.at[kind, kb],
-            dst_ref=face_recv.at[kind, kb],
-            send_sem=send_sem.at[kind, kb],
-            recv_sem=recv_sem.at[kind, kb],
-            device_id=device,
+            src_ref=face_send.at[kind, chunk],
+            dst_ref=face_recv.at[kind, target],
+            send_sem=send_sem.at[kind, chunk],
+            recv_sem=recv_sem.at[kind, target],
+            device_id=dict(device, grid=jnp.where(moves, 1, jnp.where(taken, 0, grid))),
+            device_id_type=MESH,
+        )
+
+    def arrival(kind, chunk):
+        return pltpu.make_async_remote_copy(
+            src_ref=face_send.at[kind, chunk],
+            dst_ref=face_recv.at[kind, chunk],
+            send_sem=send_sem.at[kind, chunk],
+            recv_sem=recv_sem.at[kind, chunk],
+            device_id={"grid": 1 - grid},
             device_id_type=MESH,
         )
 
@@ -347,29 +402,38 @@
     def wait_recv(kind, kb):
         @pl.when(gets[kind])
         def _():
-            send(kind, kb).wait_recv()
+            arrival(kind, kb).wait_recv()
 
     def start_send(kind, kb):
         @pl.when(puts[kind])
         def _():
             send(kind, kb).start()
 
-    inv_flat = inv_v.reshape(blocks, tall * entries * cj, LANES)
-    res_flat = res_v.reshape(blocks, tall * comps * cj, LANES)
-    cpl_flat = cpl_v.reshape(blocks, tall * cj * ROWS, LANES)
-    field_flat = field_v.reshape(blocks, tall * cj * ROWS, LANES)
-    field_rows = field_v.reshape(blocks * tall * cj, ROWS, LANES)
+    inv_flat = inv_v.reshape(inv_v.shape[0] * entries * cj, LANES)
+    res_flat = res_v.reshape(res_v.shape[0] * comps * cj, LANES)
+    cpl_flat = cpl_v.reshape(cpl_v.shape[0] * cj * ROWS, LANES)
+    field_flat = field_v.reshape(field_v.shape[0] * cj * ROWS, LANES)
+    field_rows = field_v.reshape(field_v.shape[0] * cj, ROWS, LANES)
 
     def entry(ref, kb, s, height, e):
-        start = s * height * cj + e * cj + cj - 1
-        return ref[kb, pl.ds(start, cj, stride=height * cj - 1), :]
-
-    def cell_rows(s, c):
-        return pl.ds((s * cj + cj - 1) * ROWS + c, cj, stride=(cj - 1) * ROWS)
+        base = pl.multiple_of(kb * (pitch * height * cj), ROWS)
+        start = base + (s * height * cj + e * cj + cj - 1)
+        return ref[pl.ds(start, cj, stride=height * cj - 1), :]
+
+    def cell_rows(kb, s, c):
+        base = pl.multiple_of(kb * (pitch * cj * ROWS), ROWS)
+        return pl.ds(base + ((s * cj + cj - 1) * ROWS + c), cj, stride=(cj - 1) * ROWS)
 
     def forward(kb):
-        for copy in input_copies(kb):
-            copy.wait()
+        @pl.when(kb < blocks)
+        def _():
+            for copy in input_copies(kb):
+                copy.wait()
+
+        @pl.when(kb >= blocks)
+        def _():
+            for kind in range(3):
+                ship(kind, kb - blocks).wait_recv()
 
         @pl.when(kb == 0)
         def _():
@@ -383,8 +447,8 @@
         prev = [jnp.zeros((cj, LANES), jnp.float32)] * comps
         lower = [jnp.zeros((cj, LANES), jnp.float32)] * comps
         for s in range(steps):
-            coef_a = cpl_flat[kb, cell_rows(s, 0), :]
-            coef_b = cpl_flat[kb, cell_rows(s, 1), :]
+            coef_a = cpl_flat[cell_rows(kb, s, 0), :]
+            coef_b = cpl_flat[cell_rows(kb, s, 1), :]
             up = prev
             if s < cj:
                 up = [jnp.where(sub == cj - 1 - s, upper[c], prev[c]) for c in range(comps)]
@@ -425,15 +489,24 @@
         def _():
             wave_on()
 
+        @pl.when(first_core & beyond)
+        def _():
+            ship(3, kb).start()
+
     def backward(kb):
+        @pl.when((kb >= blocks) & jnp.logical_not(far))
+        def _():
+            for kind in (0, 1, 3):
+                ship(kind, kb - blocks).wait_recv()
+
         wait_recv(2, kb)
         wait_recv(3, kb)
         under = [face_recv[2, kb, pl.ds(c * ROWS, cj), :] for c in range(comps)]
         prev = [jnp.zeros((cj, LANES), jnp.float32)] * comps
         upper = [jnp.zeros((cj, LANES), jnp.float32)] * comps
         for s in reversed(range(steps)):
-            coef_e = cpl_flat[kb, cell_rows(s, 2), :]
-            coef_f = cpl_flat[kb, cell_rows(s, 3), :]
+            coef_e = cpl_flat[cell_rows(kb, s, 2), :]
+            coef_f = cpl_flat[cell_rows(kb, s, 3), :]
             down = prev
             if s >= ci - 1:
                 down = [
@@ -455,7 +528,7 @@
             prev = product(lambda e: entry(inv_flat, kb, s, entries, e), vec)
             prev = [star_v[kb, s, c] + prev[c] for c in range(comps)]
             for c in range(comps):
-                field_flat[kb, cell_rows(s, c), :] = prev[c]
+                field_flat[cell_rows(kb, s, c), :] = prev[c]
                 if s < cj:
                     upper[c] = jnp.where(sub == cj - 1 - s, prev[c], upper[c])
                 if s < ci:
@@ -465,17 +538,37 @@
         start_send(2, kb)
         start_send(3, kb)
 
-    middle = blocks + 1
-    last = 2 * blocks + 2
-    begin = jnp.where(ahead == reach, 1, blocks + 2)
-    early = ahead * 3 <= reach
+        @pl.when(kb >= blocks)
+        def _():
+            ship(4, kb - blocks).start()
+
+    middle = 2 * blocks + 1
+    last = 4 * blocks + 2
+    begin = jnp.where(ahead == reach, 1, middle + 1)
+    early = (ahead * 3 <= reach) | (first_core & beyond)
     asks_first = ahead * 3 >= reach * 2
+
+    def ship_inputs():
+        for kb in range(blocks):
+            ship(0, kb).start()
+            ship(1, kb).start()
+
+            @pl.when(far)
+            def _():
+                ship(2, kb).start()
 
     @pl.loop(0, last + 1)
     def _(n):
         @pl.when((n == 0) & wave_first)
         def _():
             enter()
+
+        @pl.when(first_core & beyond & (n == jnp.where(far, 0, middle)))
+        def _():
+            ship_inputs()
+
+        @pl.when((n == 0) & wave_first)
+        def _():
             wave_on()
 
         @pl.when(((n == 0) & idle_first) | ((n == middle) & jnp.logical_not(idle_first)))
@@ -486,17 +579,30 @@
         def _():
             send_asks()
 
-        @pl.when((n >= 1) & (n <= blocks))
-        def _():
-            forward(n - 1)
-
-        @pl.when((n >= begin) & (n < begin + blocks))
-        def _():
-            backward(n - begin)
+        ahead_chunk = n - 1
+        own = (ahead_chunk >= 0) & (ahead_chunk < blocks) & own_forward
+        taken = (ahead_chunk >= blocks) & (ahead_chunk < 2 * blocks) & taken_forward
+
+        @pl.when(own | taken)
+        def _():
+            forward(ahead_chunk)
+
+        back_chunk = n - begin
+        own = (back_chunk >= 0) & (back_chunk < blocks) & own_backward
+        taken = (back_chunk >= blocks) & (back_chunk < 2 * blocks) & taken_backward
+
+        @pl.when(own | taken)
+        def _():
+            backward(back_chunk)
 
         @pl.when(((n == middle) & early) | ((n == last) & jnp.logical_not(early)))
         def _():
             prepare()
+
+    @pl.when(first_core & beyond)
+    def _():
+        for kb in range(blocks):
+            ship(4, kb).wait_recv()
 
     lane8 = lax.broadcasted_iota(jnp.int32, (ROWS, LANES), 1)
 
@@ -540,12 +646,31 @@
         ask(q).wait_send()
         reply(q).wait_send()
 
+    for chunk in range(2 * blocks):
+        own = chunk < blocks
+        for kind in range(4):
+            if kind < 2:
+                done = own_forward if own else taken_forward
+            else:
+                done = own_backward if own else taken_backward
+
+            @pl.when(puts[kind] & done)
+            def _():
+                send(kind, chunk).wait_send()
+
     for kb in range(blocks):
-        for kind in range(4):
-
-            @pl.when(puts[kind])
+        for kind in range(5):
+            sent = (
+                first_core & beyond,
+                first_core & beyond,
+                first_core & far,
+                first_core & beyond & jnp.logical_not(far),
+                taken_backward,
+            )[kind]
+
+            @pl.when(sent)
             def _():
-                send(kind, kb).wait_send()
+                ship(kind, kb).wait_send()
 
 
 def run_sweeps(residual, inverses, couplings, owners, donors, weights, receptors):
@@ -554,7 +679,7 @@
     many, count = donors.shape
     blocks = length // LANES
     steps = ci + cj - 1
-    tall = ci + 2 * (cj - 1)
+    tall = 2 * blocks * (ci + cj - 1) + cj - 1
     rows, cols = lax.axis_size("px"), lax.axis_size("py")
     owner_count = rows * cols
     slot_count = max(2, 2 * count // owner_count)
@@ -569,7 +694,7 @@
     return pl.pallas_call(
         functools.partial(sweep_kernel, dims),
         out_shape=(
-            pltpu.VMEM((blocks, tall, cj, ROWS, LANES), jnp.float32),
+            pltpu.VMEM((tall, cj, ROWS, LANES), jnp.float32),
             pltpu.VMEM((1, slots), jnp.int32),
             pltpu.VMEM((owner_count, ROWS, LANES), jnp.float32),
         ),
@@ -580,12 +705,12 @@
             pltpu.VMEM(donors.shape, donors.dtype),
             pltpu.VMEM(weights.shape, weights.dtype),
             pltpu.VMEM(receptors.shape, receptors.dtype),
-            pltpu.VMEM((blocks, tall, comps * comps, cj, LANES), jnp.float32),
-            pltpu.VMEM((blocks, tall, comps, cj, LANES), jnp.float32),
-            pltpu.VMEM((blocks, tall, cj, ROWS, LANES), jnp.float32),
-            pltpu.VMEM((blocks, steps, comps, cj, LANES), jnp.float32),
-            pltpu.VMEM((4, blocks, face, LANES), jnp.float32),
-            pltpu.VMEM((4, blocks, face, LANES), jnp.float32),
+            pltpu.VMEM((tall, comps * comps, cj, LANES), jnp.float32),
+            pltpu.VMEM((tall, comps, cj, LANES), jnp.float32),
+            pltpu.VMEM((tall, cj, ROWS, LANES), jnp.float32),
+            pltpu.VMEM((2 * blocks, steps, comps, cj, LANES), jnp.float32),
+            pltpu.VMEM((4, 2 * blocks, face, LANES), jnp.float32),
+            pltpu.VMEM((4, 2 * blocks, face, LANES), jnp.float32),
             pltpu.VMEM((owner_count, ROWS, LANES), jnp.float32),
             pltpu.VMEM((owner_count, ROWS, LANES), jnp.float32),
             pltpu.VMEM((owner_count * ROWS, LANES), jnp.int32),
@@ -595,8 +720,10 @@
             pltpu.VMEM((owner_count, ROWS, LANES), jnp.float32),
             dma((3, blocks)),
             dma((4,)),
-            dma((4, blocks)),
-            dma((4, blocks)),
+            dma((4, 2 * blocks)),
+            dma((4, 2 * blocks)),
+            dma((5, blocks)),
+            dma((5, blocks)),
             dma((owner_count,)),
             dma((owner_count,)),
             dma((owner_count,)),
@@ -605,7 +732,7 @@
             pltpu.SemaphoreType.REGULAR((4,)),
         ],
         compiler_params=pltpu.CompilerParams(
-            collective_id=0, has_side_effects=True, vmem_limit_bytes=40 * 1024 * 1024
+            collective_id=0, has_side_effects=True, vmem_limit_bytes=53 * 1024 * 1024
         ),
     )(*(pltpu.with_memory_space_constraint(x, pltpu.HBM) for x in inputs))
 
@@ -613,9 +740,10 @@
 def place_kernel(dims, code, reply, field, out, work):
     ci, cj, comps, slot_count = dims
     owner_count = reply.shape[0]
-    blocks, tall = field.shape[:2]
+    blocks = out.shape[3] // LANES
+    pitch = ci + cj - 1
     lane = lax.broadcasted_iota(jnp.int32, (ROWS, LANES), 1)
-    lines = work.reshape(blocks * tall * cj, ROWS, LANES)
+    lines = work.reshape(work.shape[0] * cj, ROWS, LANES)
 
     @pl.loop(0, owner_count)
     def _(q):
@@ -625,25 +753,24 @@
             value = jnp.broadcast_to(tile[:, s : s + 1], (ROWS, LANES))
             pltpu.store(lines.at[line], value, mask=lane == spot)
 
-    stack = work.reshape(blocks, tall, cj * ROWS, LANES)
+    stack = work.reshape(work.shape[0], cj * ROWS, LANES)
 
     @pl.loop(0, ci)
     def _(i):
         for kb in range(blocks):
             for c in range(comps):
                 out[i, c, :, kb * LANES : (kb + 1) * LANES] = stack[
-                    kb, i + cj - 1, pl.ds(c, cj, stride=ROWS), :
+                    kb * pitch + cj - 1 + i, pl.ds(c, cj, stride=ROWS), :
                 ]
 
 
-def run_place(code, reply, field, dims):
+def run_place(code, reply, field, length, dims):
     ci, cj, comps, slot_count = dims
-    blocks = field.shape[0]
     vmem = pl.BlockSpec(memory_space=pltpu.VMEM)
     return pl.pallas_call(
         functools.partial(place_kernel, dims),
         out_shape=(
-            jax.ShapeDtypeStruct((ci, comps, cj, blocks * LANES), jnp.float32),
+            jax.ShapeDtypeStruct((ci, comps, cj, length), jnp.float32),
             jax.ShapeDtypeStruct(field.shape, jnp.float32),
         ),
         in_specs=[pl.BlockSpec(memory_space=pltpu.SMEM), vmem, vmem],
@@ -667,7 +794,7 @@
         receptors.reshape(1, count),
     )
     slot_count = code.shape[1] // reply.shape[0]
-    update = run_place(code, reply, field, (ci, cj, comps, slot_count))
+    update = run_place(code, reply, field, residual.shape[4], (ci, cj, comps, slot_count))
     return update.transpose(0, 2, 1, 3)[None]
 
 

time: 60.8 us -> 59.4 us (0.977)
  Pallas kernels: 60.8 us -> 59.2 us
    pallas_call x1, Pallas kernels: 56 us -> 54.5 us  [run_sweeps(): pl.pallas_call(functools.partial(sweep_kernel, dims), out_shape=(pltpu.VM...]
where the time goes in v5:
time: 59.4 us; the launch traced here: 59.2 us
  Pallas kernels  59.2 us (100%)
    pallas_call x1, Pallas kernels, run_sweeps(): pl.pallas_call(functools.partial(sweep_kernel, dims), out_shape=(pltpu.VM...  54.5 us
    pallas_call x1, Pallas kernels, run_place(): pl.pallas_call(functools.partial(place_kernel, dims), out_shape=(jax.Shap...  4.76 us

profile of v5, /device:TPU:0, one launch (start us, length us, event | category | flops | bytes accessed | tf_op | source)
XLA Modules:
  0.0 59.2 jit_solution(11470995566805977913)
XLA Ops:
  0.0 54.5 %shard_map.73 = (f32[247,8,8,128]{3,2,1,0:T(8,128)S(1)}, s32[1,1024]{1,0:T(1,128)S(1)}, f32[16,8,128]{2,1,0:T(8,128)S(1)}) custom-call(f32[8,5,8,1024]{3,2,1,0:T(8,128)} %bitcast.19, f32[8,25,8,1024]{3,2,1,0:T(8,128)} %bitcast.18, f32[8,8,4,1024]{3,2,1,0:T(4,128)} %bitcast.20, s32[1,512]{1,0:T(1,128)} %bitcast.23, s32[8,512]{1,0:T(8,128)} %bitcast.21, ...), custom_call_target="tpu_custom_call" | custom-call | tf_op jit(solution)/shard_map/pallas_call | solution.py:694
  54.5 4.8 %shard_map.74 = (f32[8,5,8,1024]{3,2,1,0:T(8,128)}, f32[247,8,8,128]{3,2,1,0:T(8,128)S(1)}) custom-call(s32[1,1024]{1,0:T(1,128)S(1)} %get-tuple-element.9.code, f32[16,8,128]{2,1,0:T(8,128)S(1)} %get-tuple-element.10.reply, f32[247,8,8,128]{3,2,1,0:T(8,128)S(1)} %get-tuple-element.11.field), custom_call_target="tpu_custom_call", output_to_operand_aliasing={{1}: (2, {})} | custom-call | tf_op jit(solution)/shard_map/pallas_call | solution.py:770

commit v6 on v5

--- a/solution.py
+++ b/solution.py
@@ -82,7 +82,7 @@
     second_core = grid == 1
 
     def is_far(at):
-        return at * 2 >= reach
+        return at * 3 >= reach * 2
 
     def is_beyond(at):
         return at >= 1
@@ -335,7 +335,7 @@
             row = kb * (pitch * cj) + (i + (cj - 1)) * cj + j
             rows_v[pl.ds(pl.multiple_of(q * ROWS, ROWS), ROWS), :] = jnp.clip(
                 row, 0, field_v.shape[0] * cj - 1
-            )
+            ) * ROWS
             turned = tile.T
             first = pl.multiple_of(q * slot_count, slot_count)
             for d in range(many):
@@ -413,7 +413,6 @@
     res_flat = res_v.reshape(res_v.shape[0] * comps * cj, LANES)
     cpl_flat = cpl_v.reshape(cpl_v.shape[0] * cj * ROWS, LANES)
     field_flat = field_v.reshape(field_v.shape[0] * cj * ROWS, LANES)
-    field_rows = field_v.reshape(field_v.shape[0] * cj, ROWS, LANES)
 
     def entry(ref, kb, s, height, e):
         base = pl.multiple_of(kb * (pitch * height * cj), ROWS)
@@ -546,7 +545,7 @@
     last = 4 * blocks + 2
     begin = jnp.where(ahead == reach, 1, middle + 1)
     early = (ahead * 3 <= reach) | (first_core & beyond)
-    asks_first = ahead * 3 >= reach * 2
+    asks_first = far | (second_core & (ahead * 2 >= reach))
 
     def ship_inputs():
         for kb in range(blocks):
@@ -563,7 +562,7 @@
         def _():
             enter()
 
-        @pl.when(first_core & beyond & (n == jnp.where(far, 0, middle)))
+        @pl.when(first_core & beyond & (n == 0))
         def _():
             ship_inputs()
 
@@ -610,7 +609,7 @@
         acc = jnp.zeros((ROWS, LANES), jnp.float32)
         for s in range(slot_count):
             parts = [
-                field_rows[rows_s[slot, d, s]] * spread[d, pl.ds(q * slot_count + s, 1), :]
+                field_flat[pl.ds(rows_s[slot, d, s], ROWS), :] * spread[d, pl.ds(q * slot_count + s, 1), :]
                 for d in range(many)
             ]
             while len(parts) > 1:

time: 59.4 us -> 58.6 us (0.987)
  Pallas kernels: 59.2 us -> 58.4 us
    pallas_call x1, Pallas kernels: 54.5 us -> 53.6 us  [run_sweeps(): pl.pallas_call(functools.partial(sweep_kernel, dims), out_shape=(pltpu.VM...]
where the time goes in v6:
time: 58.6 us; the launch traced here: 58.4 us
  Pallas kernels  58.4 us (100%)
    pallas_call x1, Pallas kernels, run_sweeps(): pl.pallas_call(functools.partial(sweep_kernel, dims), out_shape=(pltpu.VM...  53.6 us
    pallas_call x1, Pallas kernels, run_place(): pl.pallas_call(functools.partial(place_kernel, dims), out_shape=(jax.Shap...  4.76 us

profile of v6, /device:TPU:0, one launch (start us, length us, event | category | flops | bytes accessed | tf_op | source)
XLA Modules:
  0.0 58.4 jit_solution(10207842298199299662)
XLA Ops:
  0.0 53.6 %shard_map.73 = (f32[247,8,8,128]{3,2,1,0:T(8,128)S(1)}, s32[1,1024]{1,0:T(1,128)S(1)}, f32[16,8,128]{2,1,0:T(8,128)S(1)}) custom-call(f32[8,5,8,1024]{3,2,1,0:T(8,128)} %bitcast.19, f32[8,25,8,1024]{3,2,1,0:T(8,128)} %bitcast.18, f32[8,8,4,1024]{3,2,1,0:T(4,128)} %bitcast.20, s32[1,512]{1,0:T(1,128)} %bitcast.23, s32[8,512]{1,0:T(8,128)} %bitcast.21, ...), custom_call_target="tpu_custom_call" | custom-call | tf_op jit(solution)/shard_map/pallas_call | solution.py:693
  53.6 4.8 %shard_map.74 = (f32[8,5,8,1024]{3,2,1,0:T(8,128)}, f32[247,8,8,128]{3,2,1,0:T(8,128)S(1)}) custom-call(s32[1,1024]{1,0:T(1,128)S(1)} %get-tuple-element.9.code, f32[16,8,128]{2,1,0:T(8,128)S(1)} %get-tuple-element.10.reply, f32[247,8,8,128]{3,2,1,0:T(8,128)S(1)} %get-tuple-element.11.field), custom_call_target="tpu_custom_call", output_to_operand_aliasing={{1}: (2, {})} | custom-call | tf_op jit(solution)/shard_map/pallas_call | solution.py:769

commit v7 on v6

--- a/solution.py
+++ b/solution.py
@@ -343,6 +343,12 @@
                 share = turned[slot_count : 2 * slot_count, d : d + 1]
                 spread[d, pl.ds(first, slot_count), :] = jnp.where(line == spot, share, 0.0)
 
+        for slot in range(FETCHES - 1):
+            fetch_rows(turn_of(slot), slot).start()
+
+    def turn_of(t):
+        return (me + (owner_count - 1) - t) % owner_count
+
     def fetch_rows(q, slot):
         return pltpu.make_async_copy(
             rows_v.at[pl.ds(pl.multiple_of(q * ROWS, ROWS), ROWS)],
@@ -619,26 +625,18 @@
         reply_send[q] = acc
         reply(q).start()
 
-    for slot in range(FETCHES - 1):
-        fetch_rows(slot, slot).start()
-
     @pl.loop(0, owner_count // FETCHES)
     def _(turn):
         for slot in range(FETCHES):
-            q = turn * FETCHES + slot
-            following = q + FETCHES - 1
+            t = turn * FETCHES + slot
+            following = t + FETCHES - 1
 
             @pl.when(following < owner_count)
             def _():
-                fetch_rows(following, (slot + FETCHES - 1) % FETCHES).start()
-
-            fetch_rows(q, slot).wait()
-            gather(q, slot)
-
-    @pl.loop(0, owner_count)
-    def _(q):
-        replied(q).wait_recv()
-        reply_out[q] = reply_recv[q]
+                fetch_rows(turn_of(following), (slot + FETCHES - 1) % FETCHES).start()
+
+            fetch_rows(turn_of(t), slot).wait()
+            gather(turn_of(t), slot)
 
     @pl.loop(0, owner_count)
     def _(q):
@@ -670,6 +668,11 @@
             @pl.when(sent)
             def _():
                 ship(kind, kb).wait_send()
+
+    @pl.loop(0, owner_count)
+    def _(q):
+        replied(q).wait_recv()
+        reply_out[q] = reply_recv[q]
 
 
 def run_sweeps(residual, inverses, couplings, owners, donors, weights, receptors):
@@ -736,7 +739,7 @@
     )(*(pltpu.with_memory_space_constraint(x, pltpu.HBM) for x in inputs))
 
 
-def place_kernel(dims, code, reply, field, out, work):
+def place_kernel(dims, code, reply, field, out_hbm, work, out, out_sem):
     ci, cj, comps, slot_count = dims
     owner_count = reply.shape[0]
     blocks = out.shape[3] // LANES
@@ -754,6 +757,9 @@
 
     stack = work.reshape(work.shape[0], cj * ROWS, LANES)
 
+    def out_copy(i):
+        return pltpu.make_async_copy(out.at[i], out_hbm.at[i], out_sem.at[i])
+
     @pl.loop(0, ci)
     def _(i):
         for kb in range(blocks):
@@ -761,6 +767,11 @@
                 out[i, c, :, kb * LANES : (kb + 1) * LANES] = stack[
                     kb * pitch + cj - 1 + i, pl.ds(c, cj, stride=ROWS), :
                 ]
+        out_copy(i).start()
+
+    @pl.loop(0, ci)
+    def _(i):
+        out_copy(i).wait()
 
 
 def run_place(code, reply, field, length, dims):
@@ -773,7 +784,11 @@
             jax.ShapeDtypeStruct(field.shape, jnp.float32),
         ),
         in_specs=[pl.BlockSpec(memory_space=pltpu.SMEM), vmem, vmem],
-        out_specs=(vmem, vmem),
+        out_specs=(pl.BlockSpec(memory_space=pltpu.HBM), vmem),
+        scratch_shapes=[
+            pltpu.VMEM((ci, comps, cj, length), jnp.float32),
+            pltpu.SemaphoreType.DMA((ci,)),
+        ],
         input_output_aliases={2: 1},
         compiler_params=pltpu.CompilerParams(vmem_limit_bytes=16 * 1024 * 1024),
     )(code, reply, field)[0]

time: 58.6 us -> 57.3 us (0.978)
  Pallas kernels: 58.4 us -> 57.2 us
    pallas_call x1, Pallas kernels: 53.6 us -> 52.6 us  [run_sweeps(): pl.pallas_call(functools.partial(sweep_kernel, dims), out_shape=(pltpu.VM...]
where the time goes in v7:
time: 57.3 us; the launch traced here: 57.2 us
  Pallas kernels  57.2 us (100%)
    pallas_call x1, Pallas kernels, run_sweeps(): pl.pallas_call(functools.partial(sweep_kernel, dims), out_shape=(pltpu.VM...  52.6 us
    pallas_call x1, Pallas kernels, run_place(): pl.pallas_call(functools.partial(place_kernel, dims), out_shape=(jax.Shap...  4.58 us

profile of v7, /device:TPU:0, one launch (start us, length us, event | category | flops | bytes accessed | tf_op | source)
XLA Modules:
  0.0 57.2 jit_solution(7988160554203916247)
XLA Ops:
  0.0 52.6 %shard_map.73 = (f32[247,8,8,128]{3,2,1,0:T(8,128)S(1)}, s32[1,1024]{1,0:T(1,128)S(1)}, f32[16,8,128]{2,1,0:T(8,128)S(1)}) custom-call(f32[8,5,8,1024]{3,2,1,0:T(8,128)} %bitcast.19, f32[8,25,8,1024]{3,2,1,0:T(8,128)} %bitcast.18, f32[8,8,4,1024]{3,2,1,0:T(4,128)} %bitcast.20, s32[1,512]{1,0:T(1,128)} %bitcast.23, s32[8,512]{1,0:T(8,128)} %bitcast.21, ...), custom_call_target="tpu_custom_call" | custom-call | tf_op jit(solution)/shard_map/pallas_call | solution.py:696
  52.6 4.6 %shard_map.74 = (f32[8,5,8,1024]{3,2,1,0:T(8,128)}, f32[247,8,8,128]{3,2,1,0:T(8,128)S(1)}) custom-call(s32[1,1024]{1,0:T(1,128)S(1)} %get-tuple-element.9.code, f32[16,8,128]{2,1,0:T(8,128)S(1)} %get-tuple-element.10.reply, f32[247,8,8,128]{3,2,1,0:T(8,128)S(1)} %get-tuple-element.11.field), custom_call_target="tpu_custom_call", output_to_operand_aliasing={{1}: (2, {})} | custom-call | tf_op jit(solution)/shard_map/pallas_call | solution.py:780

commit v8 on v7

--- a/solution.py
+++ b/solution.py
@@ -300,7 +300,7 @@
             kb, spot = divmod_const(k, LANES)
             line = kb * (pitch * cj) + (cj - 1) * cj + pencil
             code_out[:, base : base + wide] = jnp.where(
-                mark[2:3] > 0.5, line * (2 * LANES) + spot, EMPTY
+                mark[2:3] > 0.5, line * (ROWS * 2 * LANES) + spot, EMPTY
             )
             for q in range(base // slot_count, (base + wide) // slot_count):
                 at = q * slot_count - base
@@ -745,15 +745,15 @@
     blocks = out.shape[3] // LANES
     pitch = ci + cj - 1
     lane = lax.broadcasted_iota(jnp.int32, (ROWS, LANES), 1)
-    lines = work.reshape(work.shape[0] * cj, ROWS, LANES)
-
-    @pl.loop(0, owner_count)
-    def _(q):
+    lines = work.reshape(work.shape[0] * cj * ROWS, LANES)
+
+    for q in range(owner_count):
         tile = reply[q]
         for s in range(slot_count):
             line, spot = divmod_const(code[0, q * slot_count + s], 2 * LANES)
+            rows = pl.ds(pl.multiple_of(line, ROWS), ROWS)
             value = jnp.broadcast_to(tile[:, s : s + 1], (ROWS, LANES))
-            pltpu.store(lines.at[line], value, mask=lane == spot)
+            pltpu.store(lines.at[rows], value, mask=lane == spot)
 
     stack = work.reshape(work.shape[0], cj * ROWS, LANES)
 

time: 57.3 us -> 56.5 us (0.986)
  Pallas kernels: 57.2 us -> 56.3 us
    pallas_call x1, Pallas kernels: 4.58 us -> 3.74 us  [run_place(): pl.pallas_call(functools.partial(place_kernel, dims), out_shape=(jax.Shap...]
where the time goes in v8:
time: 56.5 us; the launch traced here: 56.3 us
  Pallas kernels  56.3 us (100%)
    pallas_call x1, Pallas kernels, run_sweeps(): pl.pallas_call(functools.partial(sweep_kernel, dims), out_shape=(pltpu.VM...  52.5 us
    pallas_call x1, Pallas kernels, run_place(): pl.pallas_call(functools.partial(place_kernel, dims), out_shape=(jax.Shap...  3.74 us

profile of v8, /device:TPU:0, one launch (start us, length us, event | category | flops | bytes accessed | tf_op | source)
XLA Modules:
  0.0 56.3 jit_solution(16294969341823944574)
XLA Ops:
  0.0 52.5 %shard_map.73 = (f32[247,8,8,128]{3,2,1,0:T(8,128)S(1)}, s32[1,1024]{1,0:T(1,128)S(1)}, f32[16,8,128]{2,1,0:T(8,128)S(1)}) custom-call(f32[8,5,8,1024]{3,2,1,0:T(8,128)} %bitcast.19, f32[8,25,8,1024]{3,2,1,0:T(8,128)} %bitcast.18, f32[8,8,4,1024]{3,2,1,0:T(4,128)} %bitcast.20, s32[1,512]{1,0:T(1,128)} %bitcast.23, s32[8,512]{1,0:T(8,128)} %bitcast.21, ...), custom_call_target="tpu_custom_call" | custom-call | tf_op jit(solution)/shard_map/pallas_call | solution.py:696
  52.6 3.7 %shard_map.74 = (f32[8,5,8,1024]{3,2,1,0:T(8,128)}, f32[247,8,8,128]{3,2,1,0:T(8,128)S(1)}) custom-call(s32[1,1024]{1,0:T(1,128)S(1)} %get-tuple-element.9.code, f32[16,8,128]{2,1,0:T(8,128)S(1)} %get-tuple-element.10.reply, f32[247,8,8,128]{3,2,1,0:T(8,128)S(1)} %get-tuple-element.11.field), custom_call_target="tpu_custom_call", output_to_operand_aliasing={{1}: (2, {})} | custom-call | tf_op jit(solution)/shard_map/pallas_call | solution.py:780

commit v9 on v8

--- a/solution.py
+++ b/solution.py
@@ -747,9 +747,9 @@
     lane = lax.broadcasted_iota(jnp.int32, (ROWS, LANES), 1)
     lines = work.reshape(work.shape[0] * cj * ROWS, LANES)
 
-    for q in range(owner_count):
-        tile = reply[q]
-        for s in range(slot_count):
+    for s in range(slot_count):
+        for q in range(owner_count):
+            tile = reply[q]
             line, spot = divmod_const(code[0, q * slot_count + s], 2 * LANES)
             rows = pl.ds(pl.multiple_of(line, ROWS), ROWS)
             value = jnp.broadcast_to(tile[:, s : s + 1], (ROWS, LANES))

time: 56.5 us -> 55.7 us (0.986)
  Pallas kernels: 56.3 us -> 55.6 us
    pallas_call x1, Pallas kernels: 3.74 us -> 2.99 us  [run_place(): pl.pallas_call(functools.partial(place_kernel, dims), out_shape=(jax.Shap...]
where the time goes in v9:
time: 55.7 us; the launch traced here: 55.6 us
  Pallas kernels  55.6 us (100%)
    pallas_call x1, Pallas kernels, run_sweeps(): pl.pallas_call(functools.partial(sweep_kernel, dims), out_shape=(pltpu.VM...  52.6 us
    pallas_call x1, Pallas kernels, run_place(): pl.pallas_call(functools.partial(place_kernel, dims), out_shape=(jax.Shap...  2.99 us

profile of v9, /device:TPU:0, one launch (start us, length us, event | category | flops | bytes accessed | tf_op | source)
XLA Modules:
  0.0 55.6 jit_solution(380729003588792307)
XLA Ops:
  0.0 52.6 %shard_map.73 = (f32[247,8,8,128]{3,2,1,0:T(8,128)S(1)}, s32[1,1024]{1,0:T(1,128)S(1)}, f32[16,8,128]{2,1,0:T(8,128)S(1)}) custom-call(f32[8,5,8,1024]{3,2,1,0:T(8,128)} %bitcast.19, f32[8,25,8,1024]{3,2,1,0:T(8,128)} %bitcast.18, f32[8,8,4,1024]{3,2,1,0:T(4,128)} %bitcast.20, s32[1,512]{1,0:T(1,128)} %bitcast.23, s32[8,512]{1,0:T(8,128)} %bitcast.21, ...), custom_call_target="tpu_custom_call" | custom-call | tf_op jit(solution)/shard_map/pallas_call | solution.py:696
  52.6 3.0 %shard_map.74 = (f32[8,5,8,1024]{3,2,1,0:T(8,128)}, f32[247,8,8,128]{3,2,1,0:T(8,128)S(1)}) custom-call(s32[1,1024]{1,0:T(1,128)S(1)} %get-tuple-element.9.code, f32[16,8,128]{2,1,0:T(8,128)S(1)} %get-tuple-element.10.reply, f32[247,8,8,128]{3,2,1,0:T(8,128)S(1)} %get-tuple-element.11.field), custom_call_target="tpu_custom_call", output_to_operand_aliasing={{1}: (2, {})} | custom-call | tf_op jit(solution)/shard_map/pallas_call | solution.py:780
